TPU v7x, 16 devices: a whole 2x2x2 slice. The times are simulated.
16 devices in a mesh: fsdp: 16 (over z, y, x, core).
Axes of the slice: x: 2, y: 2, z: 2, core: 2. Of those that a mesh axis runs over, the one named last changes fastest.
Arguments:
- tok_ids: int32 [16384], P('fsdp')
- tok_labels: int32 [16384], P('fsdp')
- loss_mask: int32 [16384], P('fsdp')
- emb_table: bfloat16 [57344, 256], P('fsdp')
- gain_mlp: float32 [256], replicated
- gain_head: float32 [256], replicated
- w_gate: bfloat16 [256, 1536], P('fsdp')
- w_up: bfloat16 [256, 1536], P('fsdp')
- w_down: bfloat16 [1536, 256], P('fsdp')
Outputs:
- output 1: float32 [], replicated
- output 2: float32 [57344, 256], P('fsdp')
- output 3: float32 [256, 1536], P('fsdp')
- output 4: float32 [256, 1536], P('fsdp')
- output 5: float32 [1536, 256], P('fsdp')
All inputs are finite; a program needn't handle non-finite values.
Results may differ from a plain program's by a relative error of at most 0.00885336.
Values are sent between devices in bfloat16 or wider.
A program may use at most 1 GiB of HBM per device.

v0:
```python
import jax
import jax.numpy as jnp
from jax import lax
from jax.sharding import PartitionSpec as P

NORM_EPS = 1e-6
ROW_CONTRACT = (((1,), (1,)), ((), ()))
TOK_CONTRACT = (((0,), (0,)), ((), ()))


def rms_scale(rows_wide, norm_gain):
    inv_rms = lax.rsqrt(jnp.mean(rows_wide * rows_wide, axis=-1, keepdims=True) + NORM_EPS)
    return (rows_wide * inv_rms * norm_gain).astype(jnp.bfloat16), inv_rms


def rms_back(rows_wide, inv_rms, norm_gain, grad_out):
    scaled_grad = grad_out * norm_gain
    return inv_rms * (scaled_grad - rows_wide * (inv_rms * inv_rms) * jnp.mean(scaled_grad * rows_wide, axis=-1, keepdims=True))


def mlp_forward(emb_rows, gain_mlp, gain_head, w_gate, w_up, w_down):
    emb_wide = emb_rows.astype(jnp.float32)
    a_norm, inv_first = rms_scale(emb_wide, gain_mlp)
    gate_wide = jnp.dot(a_norm, w_gate, preferred_element_type=jnp.float32).astype(jnp.bfloat16).astype(jnp.float32)
    up_wide = jnp.dot(a_norm, w_up, preferred_element_type=jnp.float32).astype(jnp.bfloat16).astype(jnp.float32)
    gate_sig = jax.nn.sigmoid(gate_wide)
    act_rows = (gate_wide * gate_sig * up_wide).astype(jnp.bfloat16)
    hid_wide = (emb_wide + jnp.dot(act_rows, w_down, preferred_element_type=jnp.float32)).astype(jnp.bfloat16).astype(jnp.float32)
    h_norm, inv_second = rms_scale(hid_wide, gain_head)
    return (emb_wide, inv_first, a_norm, gate_wide, up_wide, gate_sig, act_rows, hid_wide, inv_second), h_norm


def head_forward(h_norm, emb_table, tok_labels, tok_coef):
    logits = lax.dot_general(h_norm, emb_table, ROW_CONTRACT, preferred_element_type=jnp.float32)
    row_max = jnp.max(logits, axis=-1, keepdims=True)
    exp_rows = jnp.exp(logits - row_max)
    sum_exp = jnp.sum(exp_rows, axis=-1, keepdims=True)
    is_label = jnp.arange(logits.shape[1])[None, :] == tok_labels[:, None]
    picked = jnp.sum(jnp.where(is_label, logits, 0.0), axis=-1)
    tok_loss = row_max[:, 0] + jnp.log(sum_exp[:, 0]) - picked
    d_logits = ((exp_rows / sum_exp - is_label.astype(jnp.float32)) * tok_coef[:, None]).astype(jnp.bfloat16)
    return jnp.sum(tok_coef * tok_loss), d_logits


def mlp_backward(saved, d_hidden, gain_mlp, w_gate, w_up, w_down):
    emb_wide, inv_first, a_norm, gate_wide, up_wide, gate_sig, act_rows = saved[:7]
    hid_grad = d_hidden.astype(jnp.bfloat16)
    d_act = lax.dot_general(hid_grad, w_down, ROW_CONTRACT, preferred_element_type=jnp.float32)
    grad_down = lax.dot_general(act_rows, hid_grad, TOK_CONTRACT, preferred_element_type=jnp.float32)
    d_up = (d_act * gate_wide * gate_sig).astype(jnp.bfloat16)
    d_gate = (d_act * up_wide * gate_sig * (1.0 + gate_wide * (1.0 - gate_sig))).astype(jnp.bfloat16)
    grad_gate = lax.dot_general(a_norm, d_gate, TOK_CONTRACT, preferred_element_type=jnp.float32)
    grad_up = lax.dot_general(a_norm, d_up, TOK_CONTRACT, preferred_element_type=jnp.float32)
    d_anorm = lax.dot_general(d_gate, w_gate, ROW_CONTRACT, preferred_element_type=jnp.float32) + lax.dot_general(d_up, w_up, ROW_CONTRACT, preferred_element_type=jnp.float32)
    grad_x = d_hidden + rms_back(emb_wide, inv_first, gain_mlp, d_anorm)
    return grad_x, grad_gate, grad_up, grad_down


def solution(mesh):
    def gather_rows(row_shard):
        return lax.all_gather(row_shard, "fsdp", axis=0, tiled=True)

    def scatter_rows(full_rows):
        return lax.psum_scatter(full_rows, "fsdp", scatter_dimension=0, tiled=True)

    def device_step(tok_ids, tok_labels, loss_mask, table_shard, gain_mlp, gain_head, gate_shard, up_shard, down_shard):
        mask_wide = loss_mask.astype(jnp.float32)
        tok_coef = mask_wide / lax.psum(jnp.sum(mask_wide), "fsdp")
        table_full = gather_rows(table_shard)
        gate_full = gather_rows(gate_shard)
        up_full = gather_rows(up_shard)
        down_full = gather_rows(down_shard)
        emb_rows = jnp.take(table_full, tok_ids, axis=0)
        saved, h_norm = mlp_forward(emb_rows, gain_mlp, gain_head, gate_full, up_full, down_full)
        loss_part, d_logits = head_forward(h_norm, table_full, tok_labels, tok_coef)
        table_again, d_logits = lax.optimization_barrier((table_shard, d_logits))
        table_back = gather_rows(table_again)
        d_hnorm = jnp.dot(d_logits, table_back, preferred_element_type=jnp.float32)
        head_grad = lax.dot_general(d_logits, h_norm, TOK_CONTRACT, preferred_element_type=jnp.float32)
        d_hidden = rms_back(saved[7], saved[8], gain_head, d_hnorm)
        gate_again, up_again, down_again, d_hidden = lax.optimization_barrier((gate_shard, up_shard, down_shard, d_hidden))
        gate_back = gather_rows(gate_again)
        up_back = gather_rows(up_again)
        down_back = gather_rows(down_again)
        grad_x, grad_gate, grad_up, grad_down = mlp_backward(saved, d_hidden, gain_mlp, gate_back, up_back, down_back)
        grad_table = head_grad + jax.ops.segment_sum(grad_x, tok_ids, num_segments=table_back.shape[0])
        return (lax.psum(loss_part, "fsdp"), scatter_rows(grad_table), scatter_rows(grad_gate), scatter_rows(grad_up), scatter_rows(grad_down))

    row_spec = P("fsdp", None)
    tok_spec = P("fsdp")
    return jax.shard_map(device_step, mesh=mesh, in_specs=(tok_spec, tok_spec, tok_spec, row_spec, P(), P(), row_spec, row_spec, row_spec), out_specs=(P(), row_spec, row_spec, row_spec, row_spec), check_vma=False)
```

profile of v0, /device:TPU:0, one launch (start us, length us, event | category | flops | bytes accessed | tf_op | source)
XLA Modules:
  0.0 1390.0 jit_solution(7107939687736622960)
XLA Ops:
  9.3 35.1 %psum.14 = f32[]{:T(128)} all-reduce(f32[]{:T(128)} %convert_reduce_fusion), channel_id=1, replica_groups=mesh['fsdp'=16] {'fsdp'}, use_global_device_ids=true, to_apply=%region_1.0 | all-reduce | flops 1 | bytes 8 | tf_op jit(solution)/shard_map/psum | solution.py:68
  45.7 16.4 %all_gather.25 = bf16[256,1536]{1,0:T(8,128)(2,1)S(1)} all-gather(bf16[16,1536]{1,0:T(8,128)(2,1)} %param.15), channel_id=1, replica_groups=mesh['fsdp'=16] {'fsdp'}, dimensions={0}, use_global_device_ids=true | all-gather | bytes 835584 | tf_op jit(solution)/shard_map/all_gather | solution.py:61
  62.1 13.9 %all_gather.26 = bf16[256,1536]{1,0:T(8,128)(2,1)S(1)} all-gather(bf16[16,1536]{1,0:T(8,128)(2,1)} %param.16), channel_id=1, replica_groups=mesh['fsdp'=16] {'fsdp'}, dimensions={0}, use_global_device_ids=true | all-gather | bytes 835584 | tf_op jit(solution)/shard_map/all_gather | solution.py:61
  76.1 15.5 %all_gather.27 = bf16[1536,256]{1,0:T(8,128)(2,1)S(1)} all-gather(bf16[96,256]{1,0:T(8,128)(2,1)} %param.17), channel_id=1, replica_groups=mesh['fsdp'=16] {'fsdp'}, dimensions={0}, use_global_device_ids=true | all-gather | bytes 835584 | tf_op jit(solution)/shard_map/all_gather | solution.py:61
  91.6 46.2 %all-gather.3.cloned.1.call-done = bf16[57344,256]{1,0:T(8,128)(2,1)} async-done(((bf16[3584,256]{1,0:T(8,128)(2,1)}), bf16[57344,256]{1,0:T(8,128)(2,1)}) %all-gather.3.cloned.1.call-update) | async-done | bytes 29360144 | tf_op jit(solution)/shard_map/all_gather | solution.py:61
  137.8 16.8 %gather_fusion = bf16[1024,256]{1,0:T(8,128)(2,1)S(1)} fusion(bf16[57344,256]{1,0:T(8,128)(2,1)} %all-gather.3.cloned.1.call-done, s32[1024]{0:T(1024)S(1)} %fusion.36), kind=kCustom, calls=%fused_computation | custom fusion | bytes 1052672 | tf_op jit(solution)/shard_map/jit(_take)/gather | solution.py:73
  156.8 3.5 fusion.1
  162.7 87.2 %fusion.45 = (f32[1024]{0:T(1024)S(1)}, f32[1024,57344]{1,0:T(8,128)}) fusion(bf16[57344,256]{1,0:T(8,128)(2,1)} %all-gather.3.cloned.1.call-done, bf16[1024,256]{0,1:T(8,128)(2,1)S(1)} %get-tuple-element.30, f32[256]{0:T(256)S(1)} %copy-done.8, f32[1024]{0:T(1024)S(1)} %get-tuple-element.26), kind=kOutput, calls=%fused_computation.74 | convolution fusion | flops 30124539904 | bytes 264774656 | tf_op jit(solution)/shard_map/dot_general | solution.py:34
  249.9 82.5 %fusion = (f32[1024]{0:T(1024)S(1)}, f32[1024]{0:T(1024)S(1)}) fusion(f32[1024,57344]{1,0:T(8,128)} %get-tuple-element.32, f32[1024]{0:T(1024)S(1)} %get-tuple-element.31, s32[1024]{0:T(1024)S(1)} %copy-done.21), kind=kLoop, calls=%fused_computation.6 | loop fusion | flops 293599232 | bytes 234897408 | tf_op jit(solution)/shard_map/reduce_sum | solution.py:37
  333.8 111.8 %multiply_convert_fusion = bf16[1024,57344]{1,0:T(8,128)(2,1)} fusion(f32[1024,57344]{1,0:T(8,128)} %get-tuple-element.32, f32[1024]{0:T(1024)S(1)} %get-tuple-element.20, f32[1024]{0:T(1024)S(1)} %get-tuple-element.17, s32[1024]{0:T(1024)S(1)} %copy-done.21, f32[1024]{0:T(1024)S(1)} %get-tuple-element.31), kind=kLoop, calls=%fused_computation.2 | loop fusion | flops 411041792 | bytes 352337920 | tf_op jit(solution)/shard_map/convert_element_type | solution.py:41
  445.7 117.7 %all-gather.5.cloned.1.call-done = bf16[57344,256]{1,0:T(8,128)(2,1)} async-done(((bf16[3584,256]{1,0:T(8,128)(2,1)}), bf16[57344,256]{1,0:T(8,128)(2,1)}) %all-gather.5.cloned.1.call-update) | async-done | bytes 29360144 | tf_op jit(solution)/shard_map/all_gather | solution.py:61
  563.4 48.3 %fusion.19 = (f32[1024]{0:T(1024)S(1)}, f32[1024,256]{0,1:T(8,128)S(1)}) fusion(bf16[1024,256]{0,1:T(8,128)(2,1)S(1)} %copy-done.4, f32[256]{0:T(256)S(1)} %copy-done.9, bf16[1024,57344]{1,0:T(8,128)(2,1)} %multiply_convert_fusion, bf16[57344,256]{1,0:T(8,128)(2,1)} %all-gather.5.cloned.1.call-done), kind=kOutput, calls=%fused_computation.44 | convolution fusion | flops 30065819648 | bytes 148378624 | tf_op jit(solution)/shard_map/dot_general | solution.py:78
  612.0 4.1 fusion.28
  616.1 14.0 %all_gather.29 = bf16[1536,256]{1,0:T(8,128)(2,1)S(1)} all-gather(bf16[96,256]{1,0:T(8,128)(2,1)S(1)} %copy-done.10), channel_id=1, replica_groups=mesh['fsdp'=16] {'fsdp'}, dimensions={0}, use_global_device_ids=true | all-gather | bytes 835584 | tf_op jit(solution)/shard_map/all_gather | solution.py:61
  630.1 6.7 fusion.10
  638.5 2.2 fusion.41
  640.8 4.1 fusion.39
  645.0 63.2 %fusion.32 = f32[57344,256]{1,0:T(8,128)} fusion(bf16[1024,57344]{1,0:T(8,128)(2,1)} %multiply_convert_fusion, bf16[1024,256]{0,1:T(8,128)(2,1)S(1)} %copy-done.4, f32[256]{0:T(256)S(1)} %copy-done.9, f32[1024]{0:T(1024)S(1)} %copy-done.7), kind=kOutput, calls=%fused_computation.58 | convolution fusion | flops 30065819648 | bytes 176690176 | tf_op jit(solution)/shard_map/dot_general | solution.py:79
  708.2 13.6 all_gather.30
  721.7 2.9 fusion.46
  724.7 13.1 all_gather.31
  739.6 43.3 %scatter_fusion = f32[57344,256]{1,0:T(8,128)} fusion(f32[57344,256]{1,0:T(8,128)} %fusion.32, s32[1024]{0:T(1024)S(1)} %copy-done.17, f32[1024,256]{1,0:T(8,128)S(1)} %copy.16), kind=kCustom, calls=%fused_computation.1 | custom fusion | flops 262144 | bytes 3149824 | tf_op jit(solution)/shard_map/scatter-add | solution.py:86
  782.8 31.6 %psum.15 = f32[]{:T(128)} all-reduce(f32[]{:T(128)} %get-tuple-element.19), channel_id=1, replica_groups=mesh['fsdp'=16] {'fsdp'}, use_global_device_ids=true, to_apply=%region_8.9 | all-reduce | flops 1 | bytes 8 | tf_op jit(solution)/shard_map/psum | solution.py:87
  814.4 568.3 %reduce-scatter.5.cloned.1.call-done = f32[3584,256]{1,0:T(8,128)} async-done(((f32[57344,256]{1,0:T(8,128)}), f32[3584,256]{1,0:T(8,128)}) %reduce-scatter.5.cloned.1.call-update) | async-done | bytes 3670032 | tf_op jit(solution)/shard_map/reduce_scatter | solution.py:64
  (83 shorter events, 13.2 us)
Async XLA Ops:
  7.2 148.5 %copy-start.22 = (f32[256]{0:T(256)S(1)}, f32[256]{0:T(256)}, u32[]{:S(2)}) copy-start(f32[256]{0:T(256)} %param.13) | copy-start | bytes 3076
  7.2 130.6 %all-gather.3.cloned.1.call-start = ((), (), s32[]{:S(2)}) async-start(), calls=%async_computation.4 | async-start | bytes 31195136 | tf_op jit(solution)/shard_map/all_gather | solution.py:61
  7.9 555.4 %all-gather.5.cloned.1.call-start = ((), (), s32[]{:S(2)}) async-start(), calls=%async_computation.5 | async-start | bytes 31195136 | tf_op jit(solution)/shard_map/all_gather | solution.py:61
  45.0 115.2 %copy-start.15 = (pred[1024]{0:T(1024)(128)(4,1)}, pred[1024]{0:T(1024)(128)(4,1)S(1)}, u32[]{:S(2)}) copy-start(pred[1024]{0:T(1024)(128)(4,1)S(1)} %compare_and_fusion) | copy-start | bytes 3076
  162.0 87.9 %copy-start.3 = (bf16[1024,256]{0,1:T(8,128)(2,1)}, bf16[1024,256]{0,1:T(8,128)(2,1)S(1)}, u32[]{:S(2)}) copy-start(bf16[1024,256]{0,1:T(8,128)(2,1)S(1)} %get-tuple-element.30) | copy-start | bytes 1572868
  162.7 87.2 %copy-start.6 = (f32[1024]{0:T(1024)}, f32[1024]{0:T(1024)S(1)}, u32[]{:S(2)}) copy-start(f32[1024]{0:T(1024)S(1)} %get-tuple-element.26) | copy-start | bytes 12292
  162.7 87.2 %copy-start.21 = (s32[1024]{0:T(1024)S(1)}, s32[1024]{0:T(1024)}, u32[]{:S(2)}) copy-start(s32[1024]{0:T(1024)} %param.10) | copy-start | bytes 12292
  249.9 82.5 %copy-start.20 = (s32[1024]{0:T(1024)S(1)}, s32[1024]{0:T(1024)}, u32[]{:S(2)}) copy-start(s32[1024]{0:T(1024)} %param.11) | copy-start | bytes 12292
  333.7 229.6 %copy-start.4 = (bf16[1024,256]{0,1:T(8,128)(2,1)S(1)}, bf16[1024,256]{0,1:T(8,128)(2,1)}, u32[]{:S(2)}) copy-start(bf16[1024,256]{0,1:T(8,128)(2,1)} %copy-done.3) | copy-start | bytes 1572868
  333.7 229.6 %copy-start.9 = (f32[256]{0:T(256)S(1)}, f32[256]{0:T(256)}, u32[]{:S(2)}) copy-start(f32[256]{0:T(256)} %param.14) | copy-start | bytes 3076
  445.6 166.1 %copy-start.7 = (f32[1024]{0:T(1024)S(1)}, f32[1024]{0:T(1024)}, u32[]{:S(2)}) copy-start(f32[1024]{0:T(1024)} %copy-done.6) | copy-start | bytes 12292
  445.6 166.1 %copy-start.19 = (f32[1024]{0:T(1024)S(1)}, f32[1024]{0:T(1024)}, u32[]{:S(2)}) copy-start(f32[1024]{0:T(1024)} %get-tuple-element.25) | copy-start | bytes 12292
  445.6 368.8 %reduce-scatter.11.cloned.1.call-start = ((), (), s32[]{:S(2)}) async-start(), calls=%async_computation.9 | async-start | bytes 1671168 | tf_op jit(solution)/shard_map/reduce_scatter | solution.py:64
  616.0 198.4 %reduce-scatter.7.cloned.1.call-start = ((), (), s32[]{:S(2)}) async-start(), calls=%async_computation.7 | async-start | bytes 1671168 | tf_op jit(solution)/shard_map/reduce_scatter | solution.py:64
  630.1 8.4 copy-start.1
  630.1 8.4 copy-start.14
  630.1 8.4 copy-start.16
  630.1 8.4 copy-start.23
  640.8 173.7 %reduce-scatter.9.cloned.1.call-start = ((), (), s32[]{:S(2)}) async-start(), calls=%async_computation.8 | async-start | bytes 1671168 | tf_op jit(solution)/shard_map/reduce_scatter | solution.py:64
  644.9 63.3 %copy-start.11 = (bf16[16,1536]{1,0:T(8,128)(2,1)S(1)}, bf16[16,1536]{1,0:T(8,128)(2,1)}, u32[]{:S(2)}) copy-start(bf16[16,1536]{1,0:T(8,128)(2,1)} %param.15) | copy-start | bytes 147460
  644.9 737.8 %reduce-scatter.5.cloned.1.call-start = ((), (), s32[]{:S(2)}) async-start(), calls=%async_computation.6 | async-start | bytes 62390272 | tf_op jit(solution)/shard_map/reduce_scatter | solution.py:64
  708.2 16.5 %copy-start.12 = (bf16[16,1536]{1,0:T(8,128)(2,1)S(1)}, bf16[16,1536]{1,0:T(8,128)(2,1)}, u32[]{:S(2)}) copy-start(bf16[16,1536]{1,0:T(8,128)(2,1)} %param.16) | copy-start | bytes 147460
  708.2 29.6 %copy-start.24 = (bf16[1024,1536]{1,0:T(8,128)(2,1)S(1)}, bf16[1024,1536]{1,0:T(8,128)(2,1)}, u32[]{:S(2)}) copy-start(bf16[1024,1536]{1,0:T(8,128)(2,1)} %get-tuple-element.21) | copy-start | bytes 9437188
  724.6 14.3 %copy-start.18 = (f32[1024]{0:T(1024)S(1)}, f32[1024]{0:T(1024)}, u32[]{:S(2)}) copy-start(f32[1024]{0:T(1024)} %get-tuple-element.23) | copy-start | bytes 12292
  (8 other events, 29.1 us)
Sparse Core Ops, SparseCore 0:
  10.2 127.5 all-gather.2
  445.7 117.5 all-gather.4
  616.2 49.3 reduce-scatter.10
  669.9 49.3 reduce-scatter.6
  723.7 49.4 reduce-scatter.8
  783.0 599.6 reduce-scatter.4
where the time goes:
time: 1400 us; the launch traced here: 1390 us
  waiting for transfers between devices  733 us (52%)
  other arithmetic  244 us (17%)
  matrix products  225 us (16%)
  blocking collectives  153 us (11%)
  local copies, waits for them, and re-layouts  19.7 us (1%)
  between operations  14.8 us (1%)
    reduce_scatter x4, waiting for transfers between devices, scatter_rows(): return lax.psum_scatter(full_rows, 'fsdp', scatter_dimension=0, tiled=True)  568 us
    all_gather x2, waiting for transfers between devices, gather_rows(): return lax.all_gather(row_shard, 'fsdp', axis=0, tiled=True)  164 us
    convert_element_type x1, other arithmetic, head_forward(): ((exp_rows / sum_exp - is_label.astype(jnp.float32)) * tok_coef[:, None])...  112 us
    dot_general x1, matrix products, head_forward(): lax.dot_general(h_norm, emb_table, ROW_CONTRACT, preferred_element_type=j...  87.2 us
    all_gather x6, blocking collectives, gather_rows(): return lax.all_gather(row_shard, 'fsdp', axis=0, tiled=True)  86.6 us
    reduce_sum x1, other arithmetic, head_forward(): sum_exp = jnp.sum(exp_rows, axis=-1, keepdims=True)  82.5 us
    dot_general x1, matrix products, device_step(): lax.dot_general(d_logits, h_norm, TOK_CONTRACT, preferred_element_type=jn...  63.2 us
    dot_general x1, matrix products, device_step(): d_hnorm = jnp.dot(d_logits, table_back, preferred_element_type=jnp.float32)  48.3 us
  transfers between devices with their start and end apart: 6, of which 3 were waited for; matrix products, arithmetic and copies ran while one was open for 9% of the time, Pallas kernels for 0%

commit v1 on v0

v1 whole, which is shorter than its diff:
```python
import functools

import jax
import jax.numpy as jnp
from jax import lax
from jax.experimental import pallas as pl
from jax.experimental.pallas import tpu as pltpu
from jax.sharding import PartitionSpec as P

NORM_EPS = 1e-6
ROW_CONTRACT = (((1,), (1,)), ((), ()))
TOK_CONTRACT = (((0,), (0,)), ((), ()))
MESH = pl.DeviceIdType.MESH
F32 = jnp.float32
BF16 = jnp.bfloat16
LOG2E = 1.4426950408889634
LN2 = 0.6931471805599453

NDEV = 16
NCHIP = 8
ROWS = 3584
TOK = 1024
DIM = 256
FF = 1536
CAP = 96
TV = 512
NT = 512
V_CHIP = 2 * ROWS
NTILE = V_CHIP // TV
NCHUNK = TOK // NT
PER_BLOCK = NTILE * NCHUNK
TOTAL = NCHIP * PER_BLOCK


def flip(chip, mask):
    out = 0
    for bit in (1, 2, 4):
        a, m = lax.rem(lax.div(chip, bit), 2), lax.rem(lax.div(mask, bit), 2)
        out = out + (a + m - 2 * a * m) * bit
    return out


def barrier_all(me):
    bar = pltpu.get_barrier_semaphore()
    for k in range(1, NDEV):
        pl.semaphore_signal(bar, inc=1, device_id=(lax.rem(me + k, NDEV),), device_id_type=MESH)
    pl.semaphore_wait(bar, NDEV - 1)


def params(cid, mib):
    return pltpu.CompilerParams(collective_id=cid, has_side_effects=True, vmem_limit_bytes=mib * 2**20)


VMEM_SPEC = pl.BlockSpec(memory_space=pltpu.VMEM)


def gather_kernel(meta, gate, up, down, meta_o, gate_o, up_o, down_o, ms, mr, ws, wr, fs, fr):
    me = lax.axis_index("fsdp")
    chip, core = lax.div(me, 2), lax.rem(me, 2)
    partner = 2 * chip + 1 - core
    barrier_all(me)
    sends = []
    for k in range(1, NDEV):
        other = lax.rem(me + k, NDEV)
        cp = pltpu.make_async_remote_copy(meta, meta_o.at[me], ms.at[k], mr.at[me], device_id=(other,), device_id_type=MESH)
        cp.start()
        sends.append(cp)
    srcs, outs = (gate, up, down), (gate_o, up_o, down_o)
    for mask in range(1, NCHIP):
        other = 2 * flip(chip, mask) + core
        for i in range(3):
            cp = pltpu.make_async_remote_copy(srcs[i], outs[i].at[me], ws.at[i, mask], wr.at[i, chip], device_id=(other,), device_id_type=MESH)
            cp.start()
            sends.append(cp)
    for i in range(3):
        cp = pltpu.make_async_remote_copy(srcs[i], outs[i].at[me], fs.at[i, chip], fr.at[i, chip], device_id=(partner,), device_id_type=MESH)
        cp.start()
        sends.append(cp)
        outs[i][me] = srcs[i][...]
    meta_o[me] = meta[...]
    for mask in range(1, NCHIP):
        there = flip(chip, mask)
        slot = 2 * there + core
        for i in range(3):
            pltpu.make_async_remote_copy(srcs[i], outs[i].at[slot], ws.at[i, mask], wr.at[i, there], device_id=(partner,), device_id_type=MESH).wait_recv()
            cp = pltpu.make_async_remote_copy(outs[i].at[slot], outs[i].at[slot], fs.at[i, there], fr.at[i, there], device_id=(partner,), device_id_type=MESH)
            cp.start()
            sends.append(cp)
    for k in range(1, NDEV):
        other = lax.rem(me + k, NDEV)
        pltpu.make_async_remote_copy(meta, meta_o.at[other], ms.at[k], mr.at[other], device_id=(other,), device_id_type=MESH).wait_recv()
    for mask in range(NCHIP):
        there = flip(chip, mask)
        for i in range(3):
            pltpu.make_async_remote_copy(srcs[i], outs[i].at[2 * there + 1 - core], fs.at[i, there], fr.at[i, there], device_id=(partner,), device_id_type=MESH).wait_recv()
    for cp in sends:
        cp.wait_send()


def gather_small(meta, gate, up, down):
    dma = pltpu.SemaphoreType.DMA
    return pl.pallas_call(
        gather_kernel,
        name="gather_small",
        out_shape=[jax.ShapeDtypeStruct((NDEV,) + a.shape, a.dtype) for a in (meta, gate, up, down)],
        in_specs=[VMEM_SPEC] * 4,
        out_specs=[VMEM_SPEC] * 4,
        scratch_shapes=[dma((NDEV,)), dma((NDEV,)), dma((3, NCHIP)), dma((3, NCHIP)), dma((3, NCHIP)), dma((3, NCHIP))],
        compiler_params=params(0, 24),
    )(meta, gate, up, down)


def send_blocks(me, send, recv, ss, rs):
    def start(k, carry):
        other = lax.rem(me + k, NDEV)
        pltpu.make_async_remote_copy(send.at[other], recv.at[me], ss.at[other], rs.at[me], device_id=(other,), device_id_type=MESH).start()
        return carry

    lax.fori_loop(1, NDEV, start, 0)


def wait_blocks(me, send, recv, ss, rs):
    def wait(k, carry):
        other = lax.rem(me + k, NDEV)
        pltpu.make_async_remote_copy(send.at[other], recv.at[other], ss.at[other], rs.at[other], device_id=(other,), device_id_type=MESH).wait()
        return carry

    lax.fori_loop(1, NDEV, wait, 0)


def rows_kernel(keys, lids, table, recv, local, send, ss, rs):
    me = lax.axis_index("fsdp")
    barrier_all(me)
    slot_iota = lax.broadcasted_iota(jnp.int32, (CAP, TOK), 0)
    for d in range(NDEV):
        hit = keys[d : d + 1, :] == slot_iota
        local[d] = jnp.sum(jnp.where(hit, lids[d : d + 1, :] + 1, 0).astype(F32), axis=1, keepdims=True)

    group = 4
    row_iota = lax.broadcasted_iota(jnp.int32, (group * CAP, 256), 1)

    def pack(g, carry):
        col = jnp.concatenate([local[g * group + j] for j in range(group)], axis=0).astype(jnp.int32)
        acc = jnp.zeros((group * CAP, DIM), F32)
        for v in range(ROWS // 256):
            pick = jnp.where(row_iota + (v * 256 + 1) == col, 1.0, 0.0).astype(BF16)
            acc = acc + jnp.dot(pick, table[v * 256 : (v + 1) * 256, :], preferred_element_type=F32)
        rows = acc.astype(BF16)
        for j in range(group):
            send[g * group + j] = rows[j * CAP : (j + 1) * CAP]
        return carry

    lax.fori_loop(0, NDEV // group, pack, 0)
    send_blocks(me, send, recv, ss, rs)
    recv[me] = send[me]
    wait_blocks(me, send, recv, ss, rs)


def fetch_rows(keys, lids, table):
    dma = pltpu.SemaphoreType.DMA
    return pl.pallas_call(
        rows_kernel,
        name="fetch_rows",
        out_shape=[jax.ShapeDtypeStruct((NDEV, CAP, DIM), BF16), jax.ShapeDtypeStruct((NDEV, CAP, 1), F32)],
        in_specs=[VMEM_SPEC] * 3,
        out_specs=[VMEM_SPEC] * 2,
        scratch_shapes=[pltpu.VMEM((NDEV, CAP, DIM), BF16), dma((NDEV,)), dma((NDEV,))],
        compiler_params=params(1, 40),
    )(keys, lids, table)


def split3(wide):
    hi = wide.astype(BF16)
    rest = wide - hi.astype(F32)
    mid = rest.astype(BF16)
    return hi, mid, (rest - mid.astype(F32)).astype(BF16)


def grads_kernel(pos, dx, recv, send, parts, ss, rs):
    me = lax.axis_index("fsdp")
    barrier_all(me)
    hi, mid, low = split3(dx[...])
    parts[:, :DIM] = hi
    parts[:, DIM : 2 * DIM] = mid
    parts[:, 2 * DIM :] = low
    slot_iota = lax.broadcasted_iota(jnp.int32, (CAP, TOK), 0)

    def pack(k, carry):
        other = lax.rem(me + k, NDEV)
        pick = jnp.where(pos[0:1, :] - other * CAP == slot_iota, 1.0, 0.0).astype(BF16)
        rows = jnp.dot(pick, parts[...], preferred_element_type=F32)
        send[other] = (rows[:, :DIM] + rows[:, DIM : 2 * DIM]) + rows[:, 2 * DIM :]

        @pl.when(k < NDEV)
        def _():
            pltpu.make_async_remote_copy(send.at[other], recv.at[me], ss.at[other], rs.at[me], device_id=(other,), device_id_type=MESH).start()

        return carry

    lax.fori_loop(1, NDEV + 1, pack, 0)
    recv[me] = send[me]
    wait_blocks(me, send, recv, ss, rs)


def send_grads(pos, dx):
    dma = pltpu.SemaphoreType.DMA
    return pl.pallas_call(
        grads_kernel,
        name="send_grads",
        out_shape=jax.ShapeDtypeStruct((NDEV, CAP, DIM), F32),
        in_specs=[VMEM_SPEC] * 2,
        out_specs=VMEM_SPEC,
        scratch_shapes=[pltpu.VMEM((NDEV, CAP, DIM), F32), pltpu.VMEM((TOK, 3 * DIM), BF16), dma((NDEV,)), dma((NDEV,))],
        compiler_params=params(2, 40),
    )(pos, dx)


def add_kernel(local, rows, base, out, parts):
    @pl.when(pl.program_id(0) == 0)
    def _():
        hi, mid, low = split3(rows[...])
        parts[:, :DIM] = hi
        parts[:, DIM : 2 * DIM] = mid
        parts[:, 2 * DIM :] = low

    first = pl.program_id(0) * 256 + 1
    iota = lax.broadcasted_iota(jnp.int32, (256, NDEV * CAP), 0) + first
    pick = jnp.where(iota == local[...], 1.0, 0.0).astype(BF16)
    sums = jnp.dot(pick, parts[...], preferred_element_type=F32)
    out[...] = base[...] + ((sums[:, :DIM] + sums[:, DIM : 2 * DIM]) + sums[:, 2 * DIM :])


def add_rows(local, rows, base):
    n = NDEV * CAP
    return pl.pallas_call(
        add_kernel,
        name="add_rows",
        grid=(ROWS // 256,),
        out_shape=jax.ShapeDtypeStruct((ROWS, DIM), F32),
        in_specs=[pl.BlockSpec((1, n), lambda i: (0, 0)), pl.BlockSpec((n, DIM), lambda i: (0, 0)), pl.BlockSpec((256, DIM), lambda i: (i, 0))],
        out_specs=pl.BlockSpec((256, DIM), lambda i: (i, 0)),
        scratch_shapes=[pltpu.VMEM((n, 3 * DIM), BF16)],
        compiler_params=pltpu.CompilerParams(vmem_limit_bytes=40 * 2**20),
    )(local.reshape(1, n).astype(jnp.int32), rows.reshape(n, DIM), base)


def reduce_kernel(gate, up, down, loss, gate_o, up_o, down_o, loss_o, pg, pu, pd, sg, su, sd, rg, ru, rd, ls, ps, pr, ss, rs, lss, lrs):
    me = lax.axis_index("fsdp")
    chip, core = lax.div(me, 2), lax.rem(me, 2)
    partner = 2 * chip + 1 - core
    barrier_all(me)
    srcs, pairs, sums, recvs, outs = (gate, up, down), (pg, pu, pd), (sg, su, sd), (rg, ru, rd), (gate_o, up_o, down_o)
    sends = []
    for i in range(3):
        cp = pltpu.make_async_remote_copy(srcs[i].at[1 - core], pairs[i], ps.at[i], pr.at[i], device_id=(partner,), device_id_type=MESH)
        cp.start()
        sends.append(cp)
    for k in range(1, NDEV):
        cp = pltpu.make_async_remote_copy(loss, ls.at[me], lss.at[k], lrs.at[me], device_id=(lax.rem(me + k, NDEV),), device_id_type=MESH)
        cp.start()
        sends.append(cp)
    ls[me] = loss[...]
    for i in range(3):
        pltpu.make_async_remote_copy(srcs[i].at[1 - core], pairs[i], ps.at[i], pr.at[i], device_id=(partner,), device_id_type=MESH).wait_recv()
        sums[i][...] = srcs[i][core] + pairs[i][...]
        for mask in range(NCHIP - 1, 0, -1):
            there = flip(chip, mask)
            cp = pltpu.make_async_remote_copy(sums[i].at[there], recvs[i].at[chip], ss.at[i, mask], rs.at[i, chip], device_id=(2 * there + core,), device_id_type=MESH)
            cp.start()
            sends.append(cp)
        recvs[i][chip] = sums[i][chip]
    for i in range(3):
        for mask in range(1, NCHIP):
            there = flip(chip, mask)
            pltpu.make_async_remote_copy(sums[i].at[there], recvs[i].at[there], ss.at[i, mask], rs.at[i, there], device_id=(2 * there + core,), device_id_type=MESH).wait_recv()
        outs[i][...] = jnp.sum(recvs[i][...], axis=0)
    for k in range(1, NDEV):
        other = lax.rem(me + k, NDEV)
        pltpu.make_async_remote_copy(loss, ls.at[other], lss.at[k], lrs.at[other], device_id=(other,), device_id_type=MESH).wait_recv()
    loss_o[...] = jnp.sum(ls[...], axis=0)
    for cp in sends:
        cp.wait_send()


def reduce_weights(gate, up, down, loss):
    dma = pltpu.SemaphoreType.DMA
    big = (gate, up, down)
    return pl.pallas_call(
        reduce_kernel,
        name="reduce_weights",
        out_shape=[jax.ShapeDtypeStruct(a.shape[2:], F32) for a in big] + [jax.ShapeDtypeStruct(loss.shape, F32)],
        in_specs=[VMEM_SPEC] * 4,
        out_specs=[VMEM_SPEC] * 4,
        scratch_shapes=[pltpu.VMEM(a.shape[1:], F32) for a in big] * 3
        + [pltpu.VMEM((NDEV,) + loss.shape, F32), dma((3,)), dma((3,)), dma((3, NCHIP)), dma((3, NCHIP)), dma((NDEV,)), dma((NDEV,))],
        compiler_params=params(3, 40),
    )(gate, up, down, loss)


def head_kernel(hn, e_own, lab, coef, dhn_o, de_o, loss_o, hn_all, e_full, e_t, d_e, dhn_buf, dhn_recv, stat, stat_recv, lse_own, lse_all, la, lb, da, db,
                hs, hr, es, er, sts, str_, lss, lsr, ds_, dr, xs, xr):
    me = lax.axis_index("fsdp")
    chip, core = lax.div(me, 2), lax.rem(me, 2)
    partner = 2 * chip + 1 - core
    bar = pltpu.get_barrier_semaphore()
    pl.semaphore_signal(bar, inc=1, device_id=(partner,), device_id_type=MESH)
    for mask in range(1, NCHIP):
        pl.semaphore_signal(bar, inc=1, device_id=(2 * flip(chip, mask) + core,), device_id_type=MESH)
    pl.semaphore_wait(bar, NCHIP)

    def same_core(there):
        return dict(device_id=(2 * there + core,), device_id_type=MESH)

    mine = pl.ds(pl.multiple_of(core * ROWS, ROWS), ROWS)
    theirs = pl.ds(pl.multiple_of((1 - core) * ROWS, ROWS), ROWS)
    e_copy = pltpu.make_async_remote_copy(e_own, e_full.at[mine], es, er, device_id=(partner,), device_id_type=MESH)
    e_copy.start()

    def hn_copy(there, slot):
        return pltpu.make_async_remote_copy(hn, hn_all.at[slot], hs.at[there], hr.at[slot], **same_core(there))

    for mask in range(1, NCHIP):
        hn_copy(flip(chip, mask), chip).start()
    e_full[mine, :] = e_own[...]
    hn_all[chip] = hn[...]
    pltpu.make_async_remote_copy(e_own, e_full.at[theirs], es, er, device_id=(partner,), device_id_type=MESH).wait()

    def where_is(g, last):
        k = lax.div(g, PER_BLOCK)
        rest = lax.rem(g, PER_BLOCK)
        n, t = lax.div(rest, NTILE), lax.rem(rest, NTILE)
        return k, flip(chip, 7 - k if last else k), pl.multiple_of(n * NT, NT), t

    def logits(g, last, out):
        _, b, n0, t = where_is(g, last)
        out[...] = lax.dot_general(e_full[pl.ds(pl.multiple_of(t * TV, TV), TV), :], hn_all[b, pl.ds(n0, NT), :], ROW_CONTRACT, preferred_element_type=F32)


    def update(tile, first, m, s):
        m = jnp.where(first, -jnp.inf, m)
        top = m
        for r in range(TV // 8):
            top = jnp.maximum(top, tile[8 * r : 8 * r + 8, :] * LOG2E)
        s = jnp.where(first, 0.0, s) * jnp.exp2(m - top)
        for r in range(TV // 8):
            s = s + jnp.exp2(tile[8 * r : 8 * r + 8, :] * LOG2E - top)
        return top, s

    logits(0, False, la)

    def pass1(i, carry):
        m, s = carry
        g = 2 * i
        _, b, n0, t = where_is(g, False)
        logits(g + 1, False, lb)
        m, s = update(la, t == 0, m, s)
        nxt = jnp.minimum(g + 2, TOTAL - 2)

        @pl.when((lax.rem(g + 2, PER_BLOCK) == 0) & (g + 2 < TOTAL))
        def _():
            _, bn, _, _ = where_is(nxt, False)
            hn_copy(bn, bn).wait_recv()

        logits(nxt, False, la)
        m, s = update(lb, False, m, s)

        @pl.when(t == NTILE - 2)
        def _():
            top = jnp.max(m, axis=0, keepdims=True)
            tot = jnp.sum(s * jnp.exp2(m - top), axis=0, keepdims=True)
            stat[b, :, pl.ds(n0, NT)] = top + jnp.log(tot) * LOG2E

        @pl.when((lax.rem(g + 2, PER_BLOCK) == 0) & (g >= PER_BLOCK))
        def _():
            pltpu.make_async_remote_copy(stat.at[b], stat_recv.at[chip], sts.at[b], str_.at[chip], **same_core(b)).start()

        return m, s

    zero = jnp.zeros((8, NT), F32)
    lax.fori_loop(0, TOTAL // 2, pass1, (zero, zero))

    stat_recv[chip] = stat[chip]

    def clear_de(i, carry):
        d_e[pl.ds(pl.multiple_of(i * 256, 256), 256), :] = jnp.zeros((256, DIM), F32)
        e_t[:, pl.ds(pl.multiple_of(i * 256, 256), 256)] = e_full[pl.ds(pl.multiple_of(i * 256, 256), 256), :].T
        return carry

    def clear_dhn(i, carry):
        dhn_buf[i] = jnp.zeros((DIM, TOK), F32)
        return carry

    for mask in range(1, NCHIP):
        there = flip(chip, mask)
        pltpu.make_async_remote_copy(stat.at[there], stat_recv.at[there], sts.at[there], str_.at[there], **same_core(there)).wait_recv()
    stats = stat_recv[...]
    top = jnp.max(stats, axis=0)
    lse_own[...] = top + jnp.log(jnp.sum(jnp.exp2(stats - top[None]), axis=0)) * LOG2E

    def lse_copy(there, slot):
        return pltpu.make_async_remote_copy(lse_own, lse_all.at[slot], lss.at[there], lsr.at[slot], **same_core(there))

    for mask in range(1, NCHIP):
        lse_copy(flip(chip, mask), chip).start()
    lse_all[chip] = lse_own[...]
    lax.fori_loop(0, V_CHIP // 256, clear_de, 0)
    lax.fori_loop(0, NCHIP, clear_dhn, 0)
    for mask in range(1, NCHIP):
        there = flip(chip, mask)
        lse_copy(there, there).wait_recv()

    iota = lax.broadcasted_iota(jnp.int32, (16, NT), 0)

    def soften(g, tile, out, acc):
        _, b, n0, t = where_is(g, True)
        c = coef[b, :, pl.ds(n0, NT)]
        shift = jnp.where(c > 0.0, lse_all[b, :, pl.ds(n0, NT)] - jnp.log(jnp.where(c > 0.0, c, 1.0)) * LOG2E, jnp.inf)
        where = lab[b, :, pl.ds(n0, NT)] - t * TV
        c = jnp.broadcast_to(c, (16, NT))
        shift = jnp.broadcast_to(shift, (16, NT))
        where = jnp.broadcast_to(where, (16, NT))
        for r in range(TV // 16):
            x = tile[16 * r : 16 * r + 16, :]
            w = jnp.where(iota + 16 * r == where, c, 0.0)
            out[16 * r : 16 * r + 16, :] = (jnp.exp2(x * LOG2E - shift) - w).astype(BF16)
            y = w * x
            acc = acc + (y[:8] + y[8:])
        return acc

    def products(g, d):
        k, b, n0, t = where_is(g, True)
        rows = pl.ds(pl.multiple_of(t * TV, TV), TV)
        d_e[rows, :] += jnp.dot(d[...], hn_all[b, pl.ds(n0, NT), :], preferred_element_type=F32)
        dhn_buf[k, :, pl.ds(n0, NT)] += jnp.dot(e_t[:, rows], d[...], preferred_element_type=F32)

    def dhn_copy(k, there, slot):
        return pltpu.make_async_remote_copy(dhn_buf.at[k], dhn_recv.at[slot], ds_.at[k], dr.at[slot], **same_core(there))

    logits(0, True, la)
    logits(1, True, lb)
    picked = soften(0, la, da, zero)

    def pass2(i, picked):
        g = 2 * i
        logits(g + 2, True, la)
        picked = soften(g + 1, lb, db, picked)
        products(g, da)
        logits(g + 3, True, lb)
        picked = soften(g + 2, la, da, picked)
        products(g + 1, db)

        @pl.when(lax.rem(g + 2, PER_BLOCK) == 0)
        def _():
            k, b, _, _ = where_is(g, True)
            dhn_copy(k, b, chip).start()

        return picked

    picked = lax.fori_loop(0, TOTAL // 2 - 1, pass2, picked)
    picked = soften(TOTAL - 1, lb, db, picked)
    products(TOTAL - 2, da)
    products(TOTAL - 1, db)

    de_recv = dhn_recv
    del de_recv

    def de_copy(rows):
        return pltpu.make_async_remote_copy(d_e.at[rows], de_o, xs, xr, device_id=(partner,), device_id_type=MESH)

    de_copy(theirs).start()
    own = coef[chip] * lse_own[...] * LN2
    loss_o[...] = jnp.zeros((8, NT), F32) - picked
    for n in range(NCHUNK):
        loss_o[0:1, :] += own[:, n * NT : (n + 1) * NT]
    for mask in range(1, NCHIP):
        there = flip(chip, mask)
        dhn_copy(7 - mask, there, there).wait_recv()
    dhn_recv[chip] = dhn_buf[7]
    total = dhn_recv[0]
    for j in range(1, NCHIP):
        total = total + dhn_recv[j]
    dhn_o[...] = total
    de_copy(theirs).wait()
    de_o[...] += d_e[mine, :]

    for mask in range(1, NCHIP):
        there = flip(chip, mask)
        hn_copy(there, chip).wait_send()
        pltpu.make_async_remote_copy(stat.at[there], stat_recv.at[chip], sts.at[there], str_.at[chip], **same_core(there)).wait_send()
        lse_copy(there, chip).wait_send()
        dhn_copy(7 - mask, there, chip).wait_send()


def head(hn, table, lab, coef):
    dma = pltpu.SemaphoreType.DMA
    vm = pltpu.VMEM
    eight = [dma((NCHIP,)), dma((NCHIP,))]
    one = [dma(()), dma(())]
    return pl.pallas_call(
        head_kernel,
        name="head",
        out_shape=[jax.ShapeDtypeStruct((DIM, TOK), F32), jax.ShapeDtypeStruct((ROWS, DIM), F32), jax.ShapeDtypeStruct((8, NT), F32)],
        in_specs=[VMEM_SPEC] * 4,
        out_specs=[VMEM_SPEC] * 3,
        scratch_shapes=[
            vm((NCHIP, TOK, DIM), BF16), vm((V_CHIP, DIM), BF16), vm((DIM, V_CHIP), BF16), vm((V_CHIP, DIM), F32),
            vm((NCHIP, DIM, TOK), F32), vm((NCHIP, DIM, TOK), F32),
            vm((NCHIP, 1, TOK), F32), vm((NCHIP, 1, TOK), F32), vm((1, TOK), F32), vm((NCHIP, 1, TOK), F32),
            vm((TV, NT), F32), vm((TV, NT), F32), vm((TV, NT), BF16), vm((TV, NT), BF16),
        ]
        + eight + one + eight + eight + eight + one,
        compiler_params=params(4, 63),
    )(hn, table, lab, coef)


def rms_scale(rows_wide, norm_gain):
    inv_rms = lax.rsqrt(jnp.mean(rows_wide * rows_wide, axis=-1, keepdims=True) + NORM_EPS)
    return (rows_wide * inv_rms * norm_gain).astype(BF16), inv_rms


def rms_back(rows_wide, inv_rms, norm_gain, grad_out):
    scaled_grad = grad_out * norm_gain
    return inv_rms * (scaled_grad - rows_wide * (inv_rms * inv_rms) * jnp.mean(scaled_grad * rows_wide, axis=-1, keepdims=True))


def mlp_forward(emb_rows, gain_mlp, gain_head, w_gate, w_up, w_down):
    emb_wide = emb_rows.astype(F32)
    a_norm, inv_first = rms_scale(emb_wide, gain_mlp)
    gate_wide = jnp.dot(a_norm, w_gate, preferred_element_type=F32).astype(BF16).astype(F32)
    up_wide = jnp.dot(a_norm, w_up, preferred_element_type=F32).astype(BF16).astype(F32)
    gate_sig = jax.nn.sigmoid(gate_wide)
    act_rows = (gate_wide * gate_sig * up_wide).astype(BF16)
    hid_wide = (emb_wide + jnp.dot(act_rows, w_down, preferred_element_type=F32)).astype(BF16).astype(F32)
    h_norm, inv_second = rms_scale(hid_wide, gain_head)
    return (emb_wide, inv_first, a_norm, gate_wide, up_wide, gate_sig, act_rows, hid_wide, inv_second), h_norm


def mlp_backward(saved, d_hidden, gain_mlp, w_gate, w_up, w_down):
    emb_wide, inv_first, a_norm, gate_wide, up_wide, gate_sig, act_rows = saved[:7]
    hid_grad = d_hidden.astype(BF16)
    d_act = lax.dot_general(hid_grad, w_down, ROW_CONTRACT, preferred_element_type=F32)
    grad_down = lax.dot_general(act_rows, hid_grad, TOK_CONTRACT, preferred_element_type=F32)
    d_up = (d_act * gate_wide * gate_sig).astype(BF16)
    d_gate = (d_act * up_wide * gate_sig * (1.0 + gate_wide * (1.0 - gate_sig))).astype(BF16)
    grad_gate = lax.dot_general(a_norm, d_gate, TOK_CONTRACT, preferred_element_type=F32)
    grad_up = lax.dot_general(a_norm, d_up, TOK_CONTRACT, preferred_element_type=F32)
    d_anorm = lax.dot_general(d_gate, w_gate, ROW_CONTRACT, preferred_element_type=F32) + lax.dot_general(d_up, w_up, ROW_CONTRACT, preferred_element_type=F32)
    grad_x = d_hidden + rms_back(emb_wide, inv_first, gain_mlp, d_anorm)
    return grad_x, grad_gate, grad_up, grad_down


def solution(mesh):
    def device_step(tok_ids, tok_labels, loss_mask, table, gain_mlp, gain_head, gate_shard, up_shard, down_shard):
        me = lax.axis_index("fsdp")
        chip, core = me // 2, me % 2
        meta = jnp.concatenate([tok_ids[None], tok_labels[None], loss_mask[None], jnp.zeros((5, TOK), jnp.int32)], axis=0)
        meta_all, gate_full, up_full, down_full = gather_small(meta, gate_shard, up_shard, down_shard)
        gate_full, up_full, down_full = gate_full.reshape(DIM, FF), up_full.reshape(DIM, FF), down_full.reshape(FF, DIM)
        ids_all = meta_all[:, 0]
        blocks = lax.dynamic_index_in_dim(meta_all.reshape(NCHIP, 2, 8, TOK), core, axis=1, keepdims=False)
        lab_rel = (blocks[:, 1] - chip * V_CHIP)[:, None, :]
        coef = blocks[:, 2].astype(F32)[:, None, :] / jnp.sum(meta_all[:, 2]).astype(F32)

        upper = jnp.triu(jnp.ones((TOK, TOK), BF16), 1)
        lids = ids_all - me * ROWS
        owned = (lids >= 0) & (lids < ROWS)
        rank = jnp.dot(owned.astype(BF16), upper, preferred_element_type=F32).astype(jnp.int32)
        key = jnp.where(owned, rank, -1)
        devices = jnp.arange(NDEV, dtype=jnp.int32)
        owner = tok_ids // ROWS
        is_owner = owner[None, :] == devices[:, None]
        my_rank = jnp.sum(jnp.where(is_owner, jnp.dot(is_owner.astype(BF16), upper, preferred_element_type=F32), 0.0), axis=0).astype(jnp.int32)
        counts = jnp.sum(((ids_all // ROWS)[:, None, :] == devices[None, :, None]).astype(jnp.int32), axis=2)
        rounds = (jnp.max(counts) + CAP - 1) // CAP
        slots = jnp.arange(NDEV * CAP, dtype=jnp.int32)

        def place(r):
            slot = my_rank - r * CAP
            return jnp.where((slot >= 0) & (slot < CAP), owner * CAP + slot, -1)

        def fetch(r):
            got, local = fetch_rows(key - r * CAP, lids, table)
            pick = (place(r)[:, None] == slots[None, :]).astype(BF16)
            return jnp.dot(pick, got.reshape(NDEV * CAP, DIM), preferred_element_type=F32).astype(BF16), local

        emb_rows, local = fetch(0)
        emb_rows = lax.fori_loop(1, rounds, lambda r, rows: rows + fetch(r)[0], emb_rows)

        saved, h_norm = mlp_forward(emb_rows, gain_mlp, gain_head, gate_full, up_full, down_full)
        d_hnorm_t, head_grad, loss_part = head(h_norm, table, lab_rel, coef)
        d_hidden = rms_back(saved[7], saved[8], gain_head, d_hnorm_t.T)
        grad_x, grad_gate, grad_up, grad_down = mlp_backward(saved, d_hidden, gain_mlp, gate_full, up_full, down_full)

        grad_table = add_rows(local, send_grads(place(0)[None], grad_x), head_grad)

        def more(r, acc):
            got = send_grads(place(r)[None], grad_x)
            slot_key = key - r * CAP
            hit = slot_key[:, None, :] == jnp.arange(CAP, dtype=jnp.int32)[None, :, None]
            where = jnp.sum(jnp.where(hit, (lids + 1)[:, None, :], 0), axis=2)
            return add_rows(where, got, acc)

        grad_table = lax.fori_loop(1, rounds, more, grad_table)
        shape_in = lambda g, rows: g.reshape(NCHIP, 2, rows, -1).transpose(1, 0, 2, 3)
        out_gate, out_up, out_down, loss = reduce_weights(shape_in(grad_gate, 16), shape_in(grad_up, 16), shape_in(grad_down, 96), loss_part)
        return jnp.sum(loss), grad_table, out_gate, out_up, out_down

    row_spec = P("fsdp", None)
    tok_spec = P("fsdp")
    return jax.shard_map(device_step, mesh=mesh, in_specs=(tok_spec, tok_spec, tok_spec, row_spec, P(), P(), row_spec, row_spec, row_spec), out_specs=(P(), row_spec, row_spec, row_spec, row_spec), check_vma=False)
```

time: 1400 us -> 428 us (0.31)
  waiting for transfers between devices: 733 us -> 0 us
  Pallas kernels: 0 us -> 382 us
  other arithmetic: 244 us -> 10.6 us
  matrix products: 225 us -> 21.8 us
  blocking collectives: 153 us -> 0 us
    reduce_scatter x4 -> x0, waiting for transfers between devices: 568 us -> none  [scatter_rows(): return lax.psum_scatter(full_rows, 'fsdp', scatter_dimension=0, tiled=True)]
    pallas_call x0 -> x6, Pallas kernels: none -> 382 us  [the longest x1 260 us: head(): pl.pallas_call(head_kernel, name='head', out_shape=[jax.ShapeDtypeStruct(...]
    dot_general x11, matrix products: 221 us -> 18.2 us  [the longest x1 4.25 us: mlp_backward(): lax.dot_general(hid_grad, w_down, ROW_CONTRACT, preferred_element_type=F32)]
    all_gather x2 -> x0, waiting for transfers between devices: 164 us -> none  [gather_rows(): return lax.all_gather(row_shard, 'fsdp', axis=0, tiled=True)]
    convert_element_type x1 -> x3, other arithmetic: 112 us -> 1.38 us  [the longest x1 1.02 us: rms_scale(): return ((rows_wide * inv_rms * norm_gain).astype(BF16), inv_rms)]
    all_gather x6 -> x0, blocking collectives: 86.6 us -> none  [gather_rows(): return lax.all_gather(row_shard, 'fsdp', axis=0, tiled=True)]
    reduce_sum x3 -> x4, other arithmetic: 85.1 us -> 3.19 us  [the longest x1 1.26 us: rms_back(): jnp.mean(scaled_grad * rows_wide, axis=-1, keepdims=True)]
    psum x2 -> x0, blocking collectives: 66.6 us -> none  [the longest x1 35.1 us: device_step(): tok_coef = mask_wide / lax.psum(jnp.sum(mask_wide), 'fsdp')]
  transfers between devices with their start and end apart: 6 -> 0, of which waited for: 3 -> 0; matrix products, arithmetic and copies ran while one was open for 9% -> 0% of each run, Pallas kernels for 0% -> 0%
where the time goes in v1:
time: 428 us; the launch traced here: 427 us
  Pallas kernels  382 us (89%)
  matrix products  21.8 us (5%)
  other arithmetic  10.6 us (2%)
  local copies, waits for them, and re-layouts  10 us (2%)
    pallas_call x1, Pallas kernels, head(): pl.pallas_call(head_kernel, name='head', out_shape=[jax.ShapeDtypeStruct(...  260 us
    pallas_call x1, Pallas kernels, reduce_weights(): pl.pallas_call(reduce_kernel, name='reduce_weights', out_shape=[jax.Shape...  36.8 us
    pallas_call x1, Pallas kernels, gather_small(): pl.pallas_call(gather_kernel, name='gather_small', out_shape=[jax.ShapeDt...  29 us
    pallas_call x1, Pallas kernels, send_grads(): pl.pallas_call(grads_kernel, name='send_grads', out_shape=jax.ShapeDtypeS...  25.9 us
    pallas_call x1, Pallas kernels, fetch_rows(): pl.pallas_call(rows_kernel, name='fetch_rows', out_shape=[jax.ShapeDtypeS...  18.8 us
    pallas_call x1, Pallas kernels, add_rows(): pl.pallas_call(add_kernel, name='add_rows', grid=(ROWS // 256,), out_shap...  12.2 us

profile of v1, /device:TPU:0, one launch (start us, length us, event | category | flops | bytes accessed | tf_op | source)
XLA Modules:
  0.0 427.1 jit_solution(6204429823495269367)
XLA Ops:
  2.0 29.0 %gather_small.1 = (s32[16,8,1024]{2,1,0:T(8,128)S(1)}, bf16[16,16,1536]{2,1,0:T(8,128)(2,1)S(1)}, bf16[16,16,1536]{2,1,0:T(8,128)(2,1)S(1)}, bf16[16,96,256]{2,1,0:T(8,128)(2,1)S(1)}) custom-call(s32[8,1024]{1,0:T(8,128)S(1)} %add_add_fusion.meta, bf16[16,1536]{1,0:T(8,128)(2,1)S(1)} %copy-done.2, bf16[16,1536]{1,0:T(8,128)(2,1)S(1)} %copy-done.3, ...), custom_call_target="tpu_custom_call" | custom-call | tf_op jit(solution)/shard_map/gather_small/pallas_call | solution.py:102
  31.0 1.0 slice_reduce_fusion
  36.4 1.2 copy-done.10
  37.6 18.8 %fetch_rows.2 = (bf16[16,96,256]{2,1,0:T(8,128)(2,1)S(1)}, f32[16,96,1]{2,1,0:T(8,128)S(1)}) custom-call(s32[16,1024]{1,0:T(8,128)S(1)} %fusion.29.keys, s32[16,1024]{1,0:T(8,128)S(1)} %get-tuple-element.335.lids, bf16[3584,256]{1,0:T(8,128)(2,1)S(1)} %copy-done.10), custom_call_target="tpu_custom_call" | custom-call | tf_op jit(solution)/shard_map/fetch_rows/pallas_call | solution.py:161
  56.3 1.9 fusion.24
  58.3 1.3 fusion.45
  60.0 2.1 convolution_convert_fusion.1
  62.2 3.8 fusion.6
  66.1 1.1 fusion.38
  68.6 1.0 fusion.40.hn
  69.6 259.5 %head.1 = (f32[256,1024]{1,0:T(8,128)}, f32[3584,256]{1,0:T(8,128)}, f32[8,512]{1,0:T(8,128)}) custom-call(bf16[1024,256]{1,0:T(8,128)(2,1)} %fusion.40.hn, bf16[3584,256]{1,0:T(8,128)(2,1)} %get-tuple-element.371, s32[8,1,1024]{2,1,0:T(1,128)} %slice_subtract_fusion.lab, f32[8,1,1024]{2,1,0:T(1,128)} %fusion.66.coef), custom_call_target="tpu_custom_call" | custom-call | tf_op jit(solution)/shard_map/head/pallas_call | solution.py:499
  329.1 1.6 copy.32
  330.8 1.3 fusion.44
  332.1 3.6 fusion.57
  336.1 4.3 fusion.15
  340.5 1.0 fusion.87
  341.5 1.1 fusion.81
  342.7 1.1 fusion.52
  343.8 1.1 fusion.79
  344.9 1.9 fusion.51.dx
  347.5 36.8 %reduce_weights.1 = (f32[16,1536]{1,0:T(8,128)S(1)}, f32[16,1536]{1,0:T(8,128)S(1)}, f32[96,256]{1,0:T(8,128)S(1)}, f32[8,512]{1,0:T(8,128)S(1)}) custom-call(f32[2,8,16,1536]{3,2,1,0:T(8,128)S(1)} %get-tuple-element.194.gate, f32[2,8,16,1536]{3,2,1,0:T(8,128)S(1)} %get-tuple-element.193.up, f32[2,8,96,256]{3,2,1,0:T(8,128)S(1)} %bitcast.68, ...), custom_call_target="tpu_custom_call" | custom-call | tf_op jit(solution)/shard_map/reduce_weights/pallas_call | solution.py:288
  385.0 25.9 %send_grads.2 = f32[16,96,256]{2,1,0:T(8,128)S(1)} custom-call(s32[1,1024]{1,0:T(1,128)S(1)} %bitcast.73, f32[1024,256]{1,0:T(8,128)} %fusion.51.dx), custom_call_target="tpu_custom_call" | custom-call | tf_op jit(solution)/shard_map/send_grads/pallas_call | solution.py:207
  410.9 2.0 copy-done.1
  412.9 12.2 %add_rows.2 = f32[3584,256]{1,0:T(8,128)} custom-call(s32[1,1536]{1,0:T(1,128)S(1)} %convert_element_type.90.local, f32[1536,256]{1,0:T(8,128)S(1)} %bitcast.67, f32[3584,256]{1,0:T(8,128)S(1)} %copy-done.1), custom_call_target="tpu_custom_call" | custom-call | tf_op jit(solution)/shard_map/add_rows/pallas_call | solution.py:235
  (73 shorter events, 10.0 us)
Async XLA Ops:
  0.6 1.2 copy-start.17
  0.6 1.3 copy-start.4
  0.7 1.3 copy-start.3
  0.7 1.3 copy-start.2
  0.7 1.2 copy-start.20
  0.7 1.2 copy-start.21
  31.0 31.1 %copy-start.6 = (bf16[16,16,1536]{2,1,0:T(8,128)(2,1)}, bf16[16,16,1536]{2,1,0:T(8,128)(2,1)S(1)}, u32[]{:S(2)}) copy-start(bf16[16,16,1536]{2,1,0:T(8,128)(2,1)S(1)} %get-tuple-element.114) | copy-start | bytes 2359300
  31.0 35.0 %copy-start.8 = (bf16[16,96,256]{2,1,0:T(8,128)(2,1)}, bf16[16,96,256]{2,1,0:T(8,128)(2,1)S(1)}, u32[]{:S(2)}) copy-start(bf16[16,96,256]{2,1,0:T(8,128)(2,1)S(1)} %get-tuple-element.115) | copy-start | bytes 2359300
  36.1 1.5 copy-start.10
  58.3 1.7 copy-start.18
  60.0 2.2 copy-start.11
  62.2 3.9 copy-start.13
  66.0 1.7 copy-start.22
  66.0 2.5 copy-start.19
  67.7 0.8 copy-start.15
  329.1 2.9 copy-start.16
  332.0 3.6 copy-start.9
  332.0 3.6 copy-start.14
  332.1 4.0 copy-start.23
  340.5 1.0 copy-start.12
  341.5 1.1 copy-start.7
  346.8 0.7 copy-start.5
  410.9 2.0 copy-start.1

commit v2 on v1

v2 whole, which is shorter than its diff:
```python
import functools

import jax
import jax.numpy as jnp
from jax import lax
from jax.experimental import pallas as pl
from jax.experimental.pallas import tpu as pltpu
from jax.sharding import PartitionSpec as P

NORM_EPS = 1e-6
ROW_CONTRACT = (((1,), (1,)), ((), ()))
TOK_CONTRACT = (((0,), (0,)), ((), ()))
MESH = pl.DeviceIdType.MESH
F32 = jnp.float32
BF16 = jnp.bfloat16
LOG2E = 1.4426950408889634
LN2 = 0.6931471805599453

NDEV = 16
NCHIP = 8
ROWS = 3584
TOK = 1024
DIM = 256
FF = 1536
CAP = 96
TV = 1024
NT = 512
V_CHIP = 2 * ROWS
NTILE = V_CHIP // TV
NCHUNK = TOK // NT
PER_BLOCK = NTILE * NCHUNK
TOTAL = NCHIP * PER_BLOCK


def flip(chip, mask):
    out = 0
    for bit in (1, 2, 4):
        a, m = lax.rem(lax.div(chip, bit), 2), lax.rem(lax.div(mask, bit), 2)
        out = out + (a + m - 2 * a * m) * bit
    return out


AXES = ((2, 4, 1), (4, 1, 2), (1, 2, 4))
OTHERS = range(1, NDEV)
MASKS = range(1, NCHIP)
COLS = 256
THREE = range(3)
EACH = (3, NCHIP)


def whereabouts():
    me = lax.axis_index("fsdp")
    chip, core = lax.div(me, 2), lax.rem(me, 2)
    return me, chip, core, me + 1 - core - core


def side(chip, bit):
    return lax.rem(lax.div(chip, bit), 2)


def turn(chip, bits):
    out = chip
    for bit in bits:
        out = out + bit * (1 - 2 * side(chip, bit))
    return out


def barrier_greet(me):
    bar = pltpu.get_barrier_semaphore()
    for k in OTHERS:
        pl.semaphore_signal(bar, inc=1, device_id=(lax.rem(me + k, NDEV),), device_id_type=MESH)


def barrier_wait():
    pl.semaphore_wait(pltpu.get_barrier_semaphore(), NDEV - 1)


def barrier_all(me):
    barrier_greet(me)
    barrier_wait()


def params(cid, mib):
    return pltpu.CompilerParams(collective_id=cid, has_side_effects=True, vmem_limit_bytes=mib * 2**20)


VMEM_SPEC = pl.BlockSpec(memory_space=pltpu.VMEM)


def pack_rows(ids_key, ids_local, table, send, local):
    slot_iota = lax.broadcasted_iota(jnp.int32, (CAP, TOK), 0)
    for d in range(NDEV):
        hit = ids_key[d : d + 1, :] == slot_iota
        local[d] = jnp.sum(jnp.where(hit, ids_local[d : d + 1, :] + 1, 0).astype(F32), axis=1, keepdims=True)

    group = 4
    row_iota = lax.broadcasted_iota(jnp.int32, (group * CAP, COLS), 1)

    def pack(g, carry):
        col = jnp.concatenate([local[g * group + j] for j in range(group)], axis=0).astype(jnp.int32)
        acc = jnp.zeros((group * CAP, DIM), F32)
        for v in range(ROWS // COLS):
            pick = jnp.where(row_iota + (v * COLS + 1) == col, 1.0, 0.0).astype(BF16)
            acc = acc + jnp.dot(pick, table[v * COLS : (v + 1) * COLS, :], preferred_element_type=F32)
        rows = acc.astype(BF16)
        for j in range(group):
            send[g * group + j] = rows[j * CAP : (j + 1) * CAP]
        return carry

    lax.fori_loop(0, NDEV // group, pack, 0)


STEP = 256


def forward_again(x, gain_mlp, gain_head, gate, up, down):
    shape = jax.ShapeDtypeStruct
    return pl.pallas_call(
        mlp_rows,
        name="forward_again",
        out_shape=[shape((TOK, DIM), BF16)] * 2,
        in_specs=[VMEM_SPEC] * 6,
        out_specs=[VMEM_SPEC] * 2,
        compiler_params=pltpu.CompilerParams(vmem_limit_bytes=48 * 2**20),
    )(x, gain_mlp, gain_head, gate, up, down)


def wide_weights(gate, up, down):
    return gate[...].reshape(DIM, FF), up[...].reshape(DIM, FF), down[...].reshape(FF, DIM)


def swiglu(a, w_gate, w_up):
    p = jnp.dot(a, w_gate, preferred_element_type=F32).astype(BF16).astype(F32)
    q = jnp.dot(a, w_up, preferred_element_type=F32).astype(BF16).astype(F32)
    sig = jax.nn.sigmoid(p)
    return p, q, sig, (p * sig * q).astype(BF16)


def mlp_rows(x, gain_mlp, gain_head, gate, up, down, h_o, hn_o):
    def some(i, carry):
        rows = pl.ds(pl.multiple_of(i * STEP, STEP), STEP)
        w_gate, w_up, w_down = wide_weights(gate, up, down)
        wide = x[rows, :].astype(F32)
        a = rms_scale(wide, gain_mlp[...])[0]
        u = swiglu(a, w_gate, w_up)[3]
        h = (wide + jnp.dot(u, w_down, preferred_element_type=F32)).astype(BF16)
        h_o[rows, :] = h
        hn_o[rows, :] = rms_scale(h.astype(F32), gain_head[...])[0]
        return carry

    lax.fori_loop(0, TOK // STEP, some, 0)


def make_upper(upper):
    for r in range(TOK // 128):
        rows = lax.broadcasted_iota(jnp.int32, (128, TOK), 0) + 128 * r
        cols = lax.broadcasted_iota(jnp.int32, (128, TOK), 1)
        upper[128 * r : 128 * r + 128, :] = jnp.where(rows < cols, 1.0, 0.0).astype(BF16)


def start_kernel(meta, gate, up, down, table, gain_mlp, gain_head, ids_o, lab_o, coef_o, pos_o, x_o, local, h_o, hn_o, gate_o, up_o, down_o,
                 meta_all, key, lid, upper, send, recv, total, ms, mr, ws, wr, fs, fr, ss, rs):
    me, chip, core, partner = whereabouts()
    barrier_greet(me)
    make_upper(upper)
    barrier_wait()
    sends = []
    for k in OTHERS:
        cp = pltpu.make_async_remote_copy(meta, meta_all.at[me], ms.at[k], mr.at[me], device_id=(lax.rem(me + k, NDEV),), device_id_type=MESH)
        cp.start()
        sends.append(cp)
    srcs, outs = (gate, up, down), (gate_o, up_o, down_o)

    def forward(i, src, slot, there):
        return pltpu.make_async_remote_copy(src, outs[i].at[slot], fs.at[i, there], fr.at[i, there], device_id=(partner,), device_id_type=MESH)

    def hop(i, stage, go):
        axes = AXES[i]
        turns = [()]
        for bit in axes[:stage]:
            turns = turns + [bits + (bit,) for bits in turns]
        across = 2 * turn(chip, axes[stage : stage + 1]) + core
        for n, bits in enumerate(turns):
            slot = len(turns) - 1 + n
            there = turn(chip, bits if go else bits + axes[stage : stage + 1])
            block = outs[i].at[2 * there + core]
            cp = pltpu.make_async_remote_copy(srcs[i] if go and not bits else block, block, ws.at[i, slot], wr.at[i, slot], device_id=(across,), device_id_type=MESH)
            if not go:
                cp.wait_recv()
                cp = forward(i, block, 2 * there + core, there)
            cp.start()
            sends.append(cp)

    for i in THREE:
        hop(i, 0, True)
    for i in THREE:
        cp = forward(i, srcs[i], me, chip)
        cp.start()
        sends.append(cp)
        outs[i][me] = srcs[i][...]
    meta_all[me] = meta[...]
    for k in OTHERS:
        other = lax.rem(me + k, NDEV)
        pltpu.make_async_remote_copy(meta, meta_all.at[other], ms.at[k], mr.at[other], device_id=(other,), device_id_type=MESH).wait_recv()

    for i in THREE:
        hop(i, 0, False)
        hop(i, 1, True)

    for d in range(NDEV):
        ids_o[d : d + 1, :] = meta_all[d, 0]
    lids = ids_o[...] - me * ROWS
    owned = (lids >= 0) & (lids < ROWS)
    rank = jnp.dot(jnp.where(owned, 1.0, 0.0).astype(BF16), upper[...], preferred_element_type=F32).astype(jnp.int32)
    key[...] = jnp.where(owned, rank, -1)
    lid[...] = lids
    with jax.named_scope("s_pack"):
        pack_rows(key, lid, table, send, local)
    send_blocks(me, send, recv, ss, rs)
    for i in THREE:
        hop(i, 1, False)
        hop(i, 2, True)
    recv[me] = send[me]

    count = meta_all[0, 2]
    for d in range(1, NDEV):
        count = count + meta_all[d, 2]
    n_all = jnp.sum(count.astype(F32), axis=1, keepdims=True)
    for j in range(NCHIP):
        lab_o[j] = meta_all[2 * j + core, 1] - chip * V_CHIP
        coef_o[j] = meta_all[2 * j + core, 2].astype(F32) / n_all

    first = lax.broadcasted_iota(jnp.int32, (NDEV, TOK), 0) * ROWS
    mine = meta[0]
    is_owner = (mine >= first) & (mine < first + ROWS)
    rank = jnp.dot(jnp.where(is_owner, 1.0, 0.0).astype(BF16), upper[...], preferred_element_type=F32).astype(jnp.int32)
    slot = jnp.where(is_owner & (rank < CAP), lax.broadcasted_iota(jnp.int32, (NDEV, TOK), 0) * CAP + rank, -1)
    pos_o[...] = jnp.max(slot, axis=0, keepdims=True)

    for i in THREE:
        hop(i, 2, False)
    with jax.named_scope("s_wait"):
        wait_blocks(me, send, recv, ss, rs)
    group = 4
    for g in range(NDEV // group):
        iota = lax.broadcasted_iota(jnp.int32, (group * CAP, TOK), 0) + g * group * CAP
        pick = jnp.where(iota == pos_o[...], 1.0, 0.0).astype(BF16)
        rows = jnp.concatenate([recv[g * group + j] for j in range(group)], axis=0)
        part = lax.dot_general(pick, rows, TOK_CONTRACT, preferred_element_type=F32)
        total[...] = part if g == 0 else total[...] + part
    x_o[...] = total[...].astype(BF16)
    for mask in range(NCHIP):
        there = flip(chip, mask)
        for i in THREE:
            forward(i, srcs[i], 2 * there + 1 - core, there).wait_recv()
    with jax.named_scope("s_mlp"):
        mlp_rows(x_o, gain_mlp, gain_head, gate_o, up_o, down_o, h_o, hn_o)
    for cp in sends:
        cp.wait_send()


def start(meta, gate, up, down, table, gain_mlp, gain_head):
    dma = pltpu.SemaphoreType.DMA
    vm = pltpu.VMEM
    shape = jax.ShapeDtypeStruct
    return pl.pallas_call(
        start_kernel,
        name="start",
        out_shape=[
            shape((NDEV, TOK), jnp.int32), shape((NCHIP, 1, TOK), jnp.int32), shape((NCHIP, 1, TOK), F32), shape((1, TOK), jnp.int32),
            shape((TOK, DIM), BF16), shape((NDEV, CAP, 1), F32),
        ]
        + [shape((TOK, DIM), BF16)] * 2
        + [shape((NDEV,) + a.shape, a.dtype) for a in (gate, up, down)],
        in_specs=[VMEM_SPEC] * 7,
        out_specs=[VMEM_SPEC] * 11,
        scratch_shapes=[
            vm((NDEV, 3, 1, TOK), jnp.int32), vm((NDEV, TOK), jnp.int32), vm((NDEV, TOK), jnp.int32), vm((TOK, TOK), BF16),
            vm((NDEV, CAP, DIM), BF16), vm((NDEV, CAP, DIM), BF16), vm((TOK, DIM), F32),
            dma((NDEV,)), dma((NDEV,)), dma(EACH), dma(EACH), dma(EACH), dma(EACH), dma((NDEV,)), dma((NDEV,)),
        ],
        compiler_params=params(0, 60),
    )(meta, gate, up, down, table, gain_mlp, gain_head)


def send_blocks(me, send, recv, ss, rs):
    def start(k, carry):
        other = lax.rem(me + k, NDEV)
        pltpu.make_async_remote_copy(send.at[other], recv.at[me], ss.at[other], rs.at[me], device_id=(other,), device_id_type=MESH).start()
        return carry

    lax.fori_loop(1, NDEV, start, 0)


def wait_blocks(me, send, recv, ss, rs):
    def wait(k, carry):
        other = lax.rem(me + k, NDEV)
        pltpu.make_async_remote_copy(send.at[other], recv.at[other], ss.at[other], rs.at[other], device_id=(other,), device_id_type=MESH).wait()
        return carry

    lax.fori_loop(1, NDEV, wait, 0)


def rows_kernel(keys, lids, table, recv, local, send, ss, rs):
    me = lax.axis_index("fsdp")
    barrier_all(me)
    pack_rows(keys, lids, table, send, local)
    send_blocks(me, send, recv, ss, rs)
    recv[me] = send[me]
    wait_blocks(me, send, recv, ss, rs)


def fetch_rows(keys, lids, table):
    dma = pltpu.SemaphoreType.DMA
    return pl.pallas_call(
        rows_kernel,
        name="fetch_rows",
        out_shape=[jax.ShapeDtypeStruct((NDEV, CAP, DIM), BF16), jax.ShapeDtypeStruct((NDEV, CAP, 1), F32)],
        in_specs=[VMEM_SPEC] * 3,
        out_specs=[VMEM_SPEC] * 2,
        scratch_shapes=[pltpu.VMEM((NDEV, CAP, DIM), BF16), dma((NDEV,)), dma((NDEV,))],
        compiler_params=params(1, 40),
    )(keys, lids, table)


def split3(wide):
    hi = wide.astype(BF16)
    rest = wide - hi.astype(F32)
    mid = rest.astype(BF16)
    return hi, mid, (rest - mid.astype(F32)).astype(BF16)


def put_parts(parts, rows, wide):
    for n, part in enumerate(split3(wide)):
        parts[rows, n * DIM : (n + 1) * DIM] = part


def add_parts(sums):
    return (sums[:, :DIM] + sums[:, DIM : 2 * DIM]) + sums[:, 2 * DIM :]


def pack_grads(me, pos, dx, send, recv, parts, ss, rs):
    put_parts(parts, slice(None), dx[...])
    slot_iota = lax.broadcasted_iota(jnp.int32, (CAP, TOK), 0)

    def pack(k, carry):
        other = lax.rem(me + k, NDEV)
        pick = jnp.where(pos[0:1, :] - other * CAP == slot_iota, 1.0, 0.0).astype(BF16)
        rows = jnp.dot(pick, parts[...], preferred_element_type=F32)
        send[other] = add_parts(rows)

        @pl.when(k < NDEV)
        def _():
            pltpu.make_async_remote_copy(send.at[other], recv.at[me], ss.at[other], rs.at[me], device_id=(other,), device_id_type=MESH).start()

        return carry

    lax.fori_loop(1, NDEV + 1, pack, 0)


def grads_kernel(pos, dx, recv, send, parts, ss, rs):
    me = lax.axis_index("fsdp")
    barrier_all(me)
    pack_grads(me, pos, dx, send, recv, parts, ss, rs)
    recv[me] = send[me]
    wait_blocks(me, send, recv, ss, rs)


def send_grads(pos, dx):
    dma = pltpu.SemaphoreType.DMA
    return pl.pallas_call(
        grads_kernel,
        name="send_grads",
        out_shape=jax.ShapeDtypeStruct((NDEV, CAP, DIM), F32),
        in_specs=[VMEM_SPEC] * 2,
        out_specs=VMEM_SPEC,
        scratch_shapes=[pltpu.VMEM((NDEV, CAP, DIM), F32), pltpu.VMEM((TOK, 3 * DIM), BF16), dma((NDEV,)), dma((NDEV,))],
        compiler_params=params(2, 40),
    )(pos, dx)


def add_kernel(local, rows, base, out, parts):
    @pl.when(pl.program_id(0) == 0)
    def _():
        put_parts(parts, slice(None), rows[...])

    first = pl.program_id(0) * COLS + 1
    iota = lax.broadcasted_iota(jnp.int32, (COLS, NDEV * CAP), 0) + first
    pick = jnp.where(iota == local[...], 1.0, 0.0).astype(BF16)
    sums = jnp.dot(pick, parts[...], preferred_element_type=F32)
    out[...] = base[...] + add_parts(sums)


def add_rows(local, rows, base):
    n = NDEV * CAP
    return pl.pallas_call(
        add_kernel,
        name="add_rows",
        grid=(ROWS // COLS,),
        out_shape=jax.ShapeDtypeStruct((ROWS, DIM), F32),
        in_specs=[pl.BlockSpec((1, n), lambda i: (0, 0)), pl.BlockSpec((n, DIM), lambda i: (0, 0)), pl.BlockSpec((COLS, DIM), lambda i: (i, 0))],
        out_specs=pl.BlockSpec((COLS, DIM), lambda i: (i, 0)),
        scratch_shapes=[pltpu.VMEM((n, 3 * DIM), BF16)],
        compiler_params=pltpu.CompilerParams(vmem_limit_bytes=40 * 2**20),
    )(local.reshape(1, n).astype(jnp.int32), rows.reshape(n, DIM), base)


def weight_grad(left, right, out):
    grad = lax.dot_general(left[...], right[...], TOK_CONTRACT, preferred_element_type=F32)
    rows = out.shape[2]
    for j in range(NDEV):
        out[j // 2, j % 2] = grad[j * rows : (j + 1) * rows]


def finish_kernel(pos, dhn, x, h, w_gate, w_up, w_down, gain_mlp, gain_head, where, base, loss, table_o, gate_o, up_o, down_o, loss_o, dx,
                  gate, up, down, dhid, dhid_b, a_all, u_all, dgate, dup, send, recv, parts, rparts, pg, pu, pd, sg, su, sd, rg, ru, rd, ls, xs, xr, ps, pr, ss, rs, lss, lrs):
    me, chip, core, partner = whereabouts()
    barrier_greet(me)
    srcs, pairs, sums, recvs, outs = (gate, up, down), (pg, pu, pd), (sg, su, sd), (rg, ru, rd), (gate_o, up_o, down_o)
    sends = []

    def pair(i):
        return pltpu.make_async_remote_copy(srcs[i].at[:, 1 - core], pairs[i], ps.at[i], pr.at[i], device_id=(partner,), device_id_type=MESH)

    def back(n, carry):
        rows = pl.ds(pl.multiple_of(n * STEP, STEP), STEP)
        wide = h[rows, :].astype(F32)
        inv = rms_scale(wide, gain_head[...])[1]
        grad = rms_back(wide, inv, gain_head[...], dhn[:, rows].T)
        dhid[rows, :] = grad
        grad = grad.astype(BF16)
        dhid_b[rows, :] = grad
        a = rms_scale(x[rows, :].astype(F32), gain_mlp[...])[0]
        a_all[rows, :] = a
        g_full, u_full, d_full = wide_weights(w_gate, w_up, w_down)
        p, q, sig, act = swiglu(a, g_full, u_full)
        u_all[rows, :] = act
        dact = lax.dot_general(grad, d_full, ROW_CONTRACT, preferred_element_type=F32)
        dup[rows, :] = (dact * p * sig).astype(BF16)
        dgate[rows, :] = (dact * q * sig * (1.0 + p * (1.0 - sig))).astype(BF16)
        return carry

    with jax.named_scope("f_back"):
        lax.fori_loop(0, TOK // STEP, back, 0)
    def hop(i, stage, go):
        b1, b2, b3 = AXES[i]
        base_1, base_2 = side(chip, b1) * b1, side(chip, b2) * b2
        if stage == 0:
            bit, blocks = b1, [(n, n // 2 * b2 + n % 2 * b3) for n in range(4)]
            lead = 0
        elif stage == 1:
            bit, blocks = b2, [(4 + n, n * b3) for n in range(2)]
            lead = base_1
        else:
            bit, blocks = b3, [(6, 0)]
            lead = base_1 + base_2
        across = 2 * turn(chip, (bit,)) + core
        for slot, rest in blocks:
            out_block = lead + (1 - side(chip, bit)) * bit + rest
            in_block = lead + side(chip, bit) * bit + rest
            cp = pltpu.make_async_remote_copy(sums[i].at[out_block], recvs[i].at[slot], ss.at[i, slot], rs.at[i, slot], device_id=(across,), device_id_type=MESH)
            if go:
                cp.start()
                sends.append(cp)
            elif stage < 2:
                cp.wait_recv()
                sums[i][in_block] = sums[i][in_block] + recvs[i][slot]
            else:
                cp.wait_recv()
                outs[i][...] = sums[i][chip] + recvs[i][slot]

    def merge(i):
        pair(i).wait()
        sums[i][...] = srcs[i][:, core] + pairs[i][...]
        hop(i, 0, True)

    def to_rows(n, carry):
        rows = pl.ds(pl.multiple_of(n * STEP, STEP), STEP)
        da = lax.dot_general(dgate[rows, :], w_gate[...].reshape(DIM, FF), ROW_CONTRACT, preferred_element_type=F32)
        da = da + lax.dot_general(dup[rows, :], w_up[...].reshape(DIM, FF), ROW_CONTRACT, preferred_element_type=F32)
        wide = x[rows, :].astype(F32)
        inv = rms_scale(wide, gain_mlp[...])[1]
        dx[rows, :] = dhid[rows, :] + rms_back(wide, inv, gain_mlp[...], da)
        return carry

    lax.fori_loop(0, TOK // STEP, to_rows, 0)
    with jax.named_scope("f_pack"):
        barrier_wait()
        pack_grads(me, pos, dx, send, recv, parts, xs, xr)
    weight_grad(u_all, dhid_b, down)
    pair(2).start()
    weight_grad(a_all, dgate, gate)
    pair(0).start()
    weight_grad(a_all, dup, up)
    pair(1).start()
    for i in (2, 0, 1):
        merge(i)
    for k in OTHERS:
        cp = pltpu.make_async_remote_copy(loss, ls.at[me], lss.at[k], lrs.at[me], device_id=(lax.rem(me + k, NDEV),), device_id_type=MESH)
        cp.start()
        sends.append(cp)
    ls[me] = loss[...]
    recv[me] = send[me]
    with jax.named_scope("f_wait"):
        wait_blocks(me, send, recv, xs, xr)
    for d in range(NDEV):
        put_parts(rparts, slice(d * CAP, (d + 1) * CAP), recv[d])

    def add(v, carry):
        rows = pl.ds(pl.multiple_of(v * NT, NT), NT)
        iota = lax.broadcasted_iota(jnp.int32, (NT, NDEV * CAP), 0) + (v * NT + 1)
        pick = jnp.where(iota == where[...], 1.0, 0.0).astype(BF16)
        got = jnp.dot(pick, rparts[...], preferred_element_type=F32)
        table_o[rows, :] = base[rows, :] + add_parts(got)
        return carry

    with jax.named_scope("f_add"):
        lax.fori_loop(0, 2, add, 0)
        for stage in (0, 1):
            for i in THREE:
                hop(i, stage, False)
                hop(i, stage + 1, True)
            lax.fori_loop(2 * stage + 2, 2 * stage + 4, add, 0)
        lax.fori_loop(6, ROWS // NT, add, 0)
    for i in THREE:
        hop(i, 2, False)
    for k in OTHERS:
        other = lax.rem(me + k, NDEV)
        pltpu.make_async_remote_copy(loss, ls.at[other], lss.at[k], lrs.at[other], device_id=(other,), device_id_type=MESH).wait_recv()
    loss_o[...] = jnp.sum(ls[...], axis=0)
    for cp in sends:
        cp.wait_send()


def finish(pos, dhn, x, h, gate, up, down, gain_mlp, gain_head, where, base, loss):
    dma = pltpu.SemaphoreType.DMA
    vm = pltpu.VMEM
    big = [jax.ShapeDtypeStruct((NCHIP, 2) + a.shape[1:], F32) for a in (gate, up, down)]
    buffers = [vm((NCHIP,) + a.shape[2:], F32) for a in big]
    back = [vm(a.shape, F32) for a in big] + [vm((TOK, DIM), F32), vm((TOK, DIM), BF16), vm((TOK, DIM), BF16), vm((TOK, FF), BF16), vm((TOK, FF), BF16), vm((TOK, FF), BF16)]
    return pl.pallas_call(
        finish_kernel,
        name="finish",
        out_shape=[jax.ShapeDtypeStruct((ROWS, DIM), F32)] + [jax.ShapeDtypeStruct(a.shape[2:], F32) for a in big] + [jax.ShapeDtypeStruct(loss.shape, F32), jax.ShapeDtypeStruct((TOK, DIM), F32)],
        in_specs=[VMEM_SPEC] * 12,
        out_specs=[VMEM_SPEC] * 6,
        scratch_shapes=back + [vm((NDEV, CAP, DIM), F32), vm((NDEV, CAP, DIM), F32), vm((TOK, 3 * DIM), BF16), vm((NDEV * CAP, 3 * DIM), BF16)]
        + buffers * 3
        + [vm((NDEV,) + loss.shape, F32), dma((NDEV,)), dma((NDEV,)), dma((3,)), dma((3,)), dma(EACH), dma(EACH), dma((NDEV,)), dma((NDEV,))],
        compiler_params=params(3, 63),
    )(pos, dhn, x, h, gate, up, down, gain_mlp, gain_head, where, base, loss)


def head_kernel(hn, e_own, lab, coef, dhn_o, de_o, loss_o, hn_all, e_full, e_t, d_e, dhn_buf, dhn_recv, stat, stat_recv, lse_own, lse_all, la, lb, da, db,
                hs, hr, es, er, sts, str_, lss, lsr, ds_, dr, xs, xr):
    me, chip, core, partner = whereabouts()
    bar = pltpu.get_barrier_semaphore()
    pl.semaphore_signal(bar, inc=1, device_id=(partner,), device_id_type=MESH)
    for mask in MASKS:
        pl.semaphore_signal(bar, inc=1, device_id=(2 * flip(chip, mask) + core,), device_id_type=MESH)
    pl.semaphore_wait(bar, NCHIP)

    def same_core(there):
        return dict(device_id=(2 * there + core,), device_id_type=MESH)

    mine = pl.ds(pl.multiple_of(core * ROWS, ROWS), ROWS)
    theirs = pl.ds(pl.multiple_of((1 - core) * ROWS, ROWS), ROWS)
    e_copy = pltpu.make_async_remote_copy(e_own, e_full.at[mine], es, er, device_id=(partner,), device_id_type=MESH)
    e_copy.start()

    def hn_copy(there, slot):
        return pltpu.make_async_remote_copy(hn, hn_all.at[slot], hs.at[there], hr.at[slot], **same_core(there))

    for mask in MASKS:
        hn_copy(flip(chip, mask), chip).start()
    e_full[mine, :] = e_own[...]
    hn_all[chip] = hn[...]
    pltpu.make_async_remote_copy(e_own, e_full.at[theirs], es, er, device_id=(partner,), device_id_type=MESH).wait()

    def where_is(g, last):
        k = lax.div(g, PER_BLOCK)
        rest = lax.rem(g, PER_BLOCK)
        n, t = lax.div(rest, NTILE), lax.rem(rest, NTILE)
        return k, flip(chip, 7 - k if last else k), pl.multiple_of(n * NT, NT), t

    def logits(g, last, out):
        _, b, n0, t = where_is(g, last)
        out[...] = lax.dot_general(e_full[pl.ds(pl.multiple_of(t * TV, TV), TV), :], hn_all[b, pl.ds(n0, NT), :], ROW_CONTRACT, preferred_element_type=F32)


    def logits_top(g, out):
        _, b, n0, t = where_is(g, False)
        tile = lax.dot_general(e_full[pl.ds(pl.multiple_of(t * TV, TV), TV), :], hn_all[b, pl.ds(n0, NT), :], ROW_CONTRACT, preferred_element_type=F32)
        out[...] = tile
        return jnp.max(tile.reshape(TV // 8, 8, NT), axis=0)

    def update(tile, tile_top, first, m, s):
        m = jnp.where(first, -jnp.inf, m)
        top = jnp.maximum(m, tile_top * LOG2E)
        sums = [jnp.where(first, 0.0, s) * jnp.exp2(m - top)] + [None] * 3
        for r in range(TV // 8):
            e = jnp.exp2(tile[8 * r : 8 * r + 8, :] * LOG2E - top)
            sums[r % 4] = e if sums[r % 4] is None else sums[r % 4] + e
        return top, (sums[0] + sums[1]) + (sums[2] + sums[3])

    def keep(g, m, s):
        _, b, n0, t = where_is(g, False)

        @pl.when(t == NTILE - 1)
        def _():
            top = jnp.max(m, axis=0, keepdims=True)
            tot = jnp.sum(s * jnp.exp2(m - top), axis=0, keepdims=True)
            stat[b, :, pl.ds(n0, NT)] = top + jnp.log(tot) * LOG2E

        @pl.when((lax.rem(g + 1, PER_BLOCK) == 0) & (g >= PER_BLOCK))
        def _():
            pltpu.make_async_remote_copy(stat.at[b], stat_recv.at[chip], sts.at[b], str_.at[chip], **same_core(b)).start()

    def pass1(i, carry):
        m, s, top_a = carry
        g = 2 * i
        nxt = jnp.minimum(g + 2, TOTAL - 2)

        @pl.when((lax.rem(g + 2, PER_BLOCK) == 0) & (g + 2 < TOTAL))
        def _():
            _, bn, _, _ = where_is(nxt, False)
            hn_copy(bn, bn).wait_recv()

        top_b = logits_top(g + 1, lb)
        ma, sa = update(la, top_a, where_is(g, False)[3] == 0, m, s)
        top_a = logits_top(nxt, la)
        mb, sb = update(lb, top_b, where_is(g + 1, False)[3] == 0, ma, sa)
        keep(g, ma, sa)
        keep(g + 1, mb, sb)
        return mb, sb, top_a

    zero = jnp.zeros((8, NT), F32)
    with jax.named_scope("pass1"):
        lax.fori_loop(0, TOTAL // 2, pass1, (zero, zero, logits_top(0, la)))

    scope = jax.named_scope("stats")
    scope.__enter__()
    stat_recv[chip] = stat[chip]

    def clear_de(i, carry):
        d_e[pl.ds(pl.multiple_of(i * COLS, COLS), COLS), :] = jnp.zeros((COLS, DIM), F32)
        e_t[:, pl.ds(pl.multiple_of(i * COLS, COLS), COLS)] = e_full[pl.ds(pl.multiple_of(i * COLS, COLS), COLS), :].T
        return carry

    def clear_dhn(i, carry):
        dhn_buf[i] = jnp.zeros((DIM, TOK), F32)
        return carry

    lax.fori_loop(0, NCHIP, clear_dhn, 0)
    for mask in MASKS:
        there = flip(chip, mask)
        pltpu.make_async_remote_copy(stat.at[there], stat_recv.at[there], sts.at[there], str_.at[there], **same_core(there)).wait_recv()
    stats = stat_recv[...]
    top = jnp.max(stats, axis=0)
    lse_own[...] = top + jnp.log(jnp.sum(jnp.exp2(stats - top[None]), axis=0)) * LOG2E

    def lse_copy(there, slot):
        return pltpu.make_async_remote_copy(lse_own, lse_all.at[slot], lss.at[there], lsr.at[slot], **same_core(there))

    for mask in MASKS:
        lse_copy(flip(chip, mask), chip).start()
    lse_all[chip] = lse_own[...]
    lax.fori_loop(0, V_CHIP // COLS, clear_de, 0)
    for mask in MASKS:
        there = flip(chip, mask)
        lse_copy(there, there).wait_recv()

    scope.__exit__(None, None, None)

    iota = lax.broadcasted_iota(jnp.int32, (16, NT), 0)

    def soften(g, tile, out, acc):
        _, b, n0, t = where_is(g, True)
        c = coef[b, :, pl.ds(n0, NT)]
        shift = jnp.where(c > 0.0, lse_all[b, :, pl.ds(n0, NT)] - jnp.log(jnp.where(c > 0.0, c, 1.0)) * LOG2E, jnp.inf)
        where = lab[b, :, pl.ds(n0, NT)] - t * TV
        c = jnp.broadcast_to(c, (16, NT))
        shift = jnp.broadcast_to(shift, (16, NT))
        where = jnp.broadcast_to(where, (16, NT))
        for r in range(TV // 16):
            x = tile[16 * r : 16 * r + 16, :]
            w = jnp.where(iota + 16 * r == where, c, 0.0)
            out[16 * r : 16 * r + 16, :] = (jnp.exp2(x * LOG2E - shift) - w).astype(BF16)
            y = w * x
            acc = acc + (y[:8] + y[8:])
        return acc

    def products(g, d):
        k, b, n0, t = where_is(g, True)
        rows = pl.ds(pl.multiple_of(t * TV, TV), TV)
        d_e[rows, :] += jnp.dot(d[...], hn_all[b, pl.ds(n0, NT), :], preferred_element_type=F32)
        dhn_buf[k, :, pl.ds(n0, NT)] += jnp.dot(e_t[:, rows], d[...], preferred_element_type=F32)

    def dhn_copy(k, there, slot):
        return pltpu.make_async_remote_copy(dhn_buf.at[k], dhn_recv.at[slot], ds_.at[k], dr.at[slot], **same_core(there))

    logits(0, True, la)
    logits(1, True, lb)
    picked = soften(0, la, da, zero)

    def pass2(i, picked):
        g = 2 * i
        logits(g + 2, True, la)
        picked = soften(g + 1, lb, db, picked)
        products(g, da)
        logits(g + 3, True, lb)
        picked = soften(g + 2, la, da, picked)
        products(g + 1, db)

        @pl.when(lax.rem(g + 2, PER_BLOCK) == 0)
        def _():
            k, b, _, _ = where_is(g, True)
            dhn_copy(k, b, chip).start()

        return picked

    with jax.named_scope("pass2"):
        picked = lax.fori_loop(0, TOTAL // 2 - 1, pass2, picked)
    picked = soften(TOTAL - 1, lb, db, picked)
    products(TOTAL - 2, da)
    products(TOTAL - 1, db)

    def de_copy(rows):
        return pltpu.make_async_remote_copy(d_e.at[rows], de_o, xs, xr, device_id=(partner,), device_id_type=MESH)

    de_copy(theirs).start()
    own = jnp.sum(coef[chip] * lse_own[...] * LN2, axis=1, keepdims=True)
    picked = jnp.sum(jnp.sum(picked, axis=0, keepdims=True), axis=1, keepdims=True)
    loss_o[...] = jnp.broadcast_to(own - picked, loss_o.shape)
    with jax.named_scope("dhn_wait"):
        for mask in MASKS:
            there = flip(chip, mask)
            dhn_copy(7 - mask, there, there).wait_recv()
    dhn_recv[chip] = dhn_buf[7]
    total = dhn_recv[0]
    for j in range(1, NCHIP):
        total = total + dhn_recv[j]
    dhn_o[...] = total
    de_copy(theirs).wait()
    de_o[...] += d_e[mine, :]

    for mask in MASKS:
        there = flip(chip, mask)
        hn_copy(there, chip).wait_send()
        pltpu.make_async_remote_copy(stat.at[there], stat_recv.at[chip], sts.at[there], str_.at[chip], **same_core(there)).wait_send()
        lse_copy(there, chip).wait_send()
        dhn_copy(7 - mask, there, chip).wait_send()


def head(hn, table, lab, coef):
    dma = pltpu.SemaphoreType.DMA
    vm = pltpu.VMEM
    eight = [dma((NCHIP,)), dma((NCHIP,))]
    one = [dma(()), dma(())]
    return pl.pallas_call(
        head_kernel,
        name="head",
        out_shape=[jax.ShapeDtypeStruct((DIM, TOK), F32), jax.ShapeDtypeStruct((ROWS, DIM), F32), jax.ShapeDtypeStruct((1, 128), F32)],
        in_specs=[VMEM_SPEC] * 4,
        out_specs=[VMEM_SPEC] * 3,
        scratch_shapes=[
            vm((NCHIP, TOK, DIM), BF16), vm((V_CHIP, DIM), BF16), vm((DIM, V_CHIP), BF16), vm((V_CHIP, DIM), F32),
            vm((NCHIP, DIM, TOK), F32), vm((NCHIP, DIM, TOK), F32),
            vm((NCHIP, 1, TOK), F32), vm((NCHIP, 1, TOK), F32), vm((1, TOK), F32), vm((NCHIP, 1, TOK), F32),
            vm((TV, NT), F32), vm((TV, NT), F32), vm((TV, NT), BF16), vm((TV, NT), BF16),
        ]
        + eight + one + eight + eight + eight + one,
        compiler_params=params(4, 63),
    )(hn, table, lab, coef)


def rms_scale(rows_wide, norm_gain):
    inv_rms = lax.rsqrt(jnp.mean(rows_wide * rows_wide, axis=-1, keepdims=True) + NORM_EPS)
    return (rows_wide * inv_rms * norm_gain).astype(BF16), inv_rms


def rms_back(rows_wide, inv_rms, norm_gain, grad_out):
    scaled_grad = grad_out * norm_gain
    return inv_rms * (scaled_grad - rows_wide * (inv_rms * inv_rms) * jnp.mean(scaled_grad * rows_wide, axis=-1, keepdims=True))


def solution(mesh):
    def device_step(tok_ids, tok_labels, loss_mask, table, gain_mlp, gain_head, gate_shard, up_shard, down_shard):
        meta = jnp.stack([tok_ids, tok_labels, loss_mask])[:, None, :]
        gains = (gain_mlp[None], gain_head[None])
        ids_all, lab_rel, coef, pos, emb_rows, local, *acts, gate_full, up_full, down_full = start(meta, gate_shard, up_shard, down_shard, table, *gains)

        devices = jnp.arange(NDEV, dtype=jnp.int32)
        counts = jnp.sum(((ids_all // ROWS)[:, None, :] == devices[None, :, None]).astype(jnp.int32), axis=2)
        rounds = (jnp.max(counts) + CAP - 1) // CAP
        slots = jnp.arange(NDEV * CAP, dtype=jnp.int32)

        def places(ids_all, tok_ids):
            upper = jnp.triu(jnp.ones((TOK, TOK), BF16), 1)
            lids = ids_all - lax.axis_index("fsdp") * ROWS
            owned = (lids >= 0) & (lids < ROWS)
            key = jnp.where(owned, jnp.dot(owned.astype(BF16), upper, preferred_element_type=F32).astype(jnp.int32), -1)
            owner = tok_ids // ROWS
            is_owner = owner[None, :] == devices[:, None]
            my_rank = jnp.sum(jnp.where(is_owner, jnp.dot(is_owner.astype(BF16), upper, preferred_element_type=F32), 0.0), axis=0).astype(jnp.int32)

            def place(r):
                slot = my_rank - r * CAP
                return jnp.where((slot >= 0) & (slot < CAP), owner * CAP + slot, -1)

            return lids, key, place

        def more_rows(rows, acts, ids_all, tok_ids, table):
            lids, key, place = places(ids_all, tok_ids)

            def one(r, rows):
                got, _ = fetch_rows(key - r * CAP, lids, table)
                pick = (place(r)[:, None] == slots[None, :]).astype(BF16)
                return rows + jnp.dot(pick, got.reshape(NDEV * CAP, DIM), preferred_element_type=F32).astype(BF16)

            rows = lax.fori_loop(1, rounds, one, rows)
            return rows, tuple(forward_again(rows, *gains, gate_full, up_full, down_full))

        emb_rows, acts = lax.cond(rounds > 1, more_rows, lambda rows, acts, *_: (rows, acts), emb_rows, tuple(acts), ids_all, tok_ids, table)
        hid, h_norm = acts
        d_hnorm_t, head_grad, loss_part = head(h_norm, table, lab_rel, coef)
        where = local.reshape(1, NDEV * CAP).astype(jnp.int32)
        grad_table, out_gate, out_up, out_down, loss, grad_x = finish(
            pos, d_hnorm_t, emb_rows, hid, gate_full, up_full, down_full, *gains, where, head_grad, loss_part
        )

        def more_grads(acc, ids_all, tok_ids, grad_x):
            lids, key, place = places(ids_all, tok_ids)

            def one(r, acc):
                got = send_grads(place(r)[None], grad_x)
                hit = (key - r * CAP)[:, None, :] == jnp.arange(CAP, dtype=jnp.int32)[None, :, None]
                return add_rows(jnp.sum(jnp.where(hit, (lids + 1)[:, None, :], 0), axis=2), got, acc)

            return lax.fori_loop(1, rounds, one, acc)

        grad_table = lax.cond(rounds > 1, more_grads, lambda acc, *_: acc, grad_table, ids_all, tok_ids, grad_x)
        return loss[0, 0], grad_table, out_gate, out_up, out_down

    row_spec = P("fsdp", None)
    tok_spec = P("fsdp")
    return jax.shard_map(device_step, mesh=mesh, in_specs=(tok_spec, tok_spec, tok_spec, row_spec, P(), P(), row_spec, row_spec, row_spec), out_specs=(P(), row_spec, row_spec, row_spec, row_spec), check_vma=False)
```

time: 428 us -> 328 us (0.77)
  Pallas kernels: 382 us -> 314 us
  matrix products: 21.8 us -> 0 us
  other arithmetic: 10.6 us -> 3.27 us
    pallas_call x1, Pallas kernels: 260 us -> 214 us  [head(): pl.pallas_call(head_kernel, name='head', out_shape=[jax.ShapeDtypeStruct(...]
    pallas_call x5 -> x2, Pallas kernels: 123 us -> 99.6 us  [the longest x1 57.9 us: finish(): pl.pallas_call(finish_kernel, name='finish', out_shape=[jax.ShapeDtypeStr...]
    dot_general x12 -> x0, matrix products: 21.8 us -> none  [the longest x1 4.25 us: mlp_backward(): lax.dot_general(hid_grad, w_down, ROW_CONTRACT, preferred_element_type=F32)]
where the time goes in v2:
time: 328 us
  Pallas kernels  314 us (96%)
  local copies, waits for them, and re-layouts  7.93 us (2%)
    pallas_call x1, Pallas kernels, head(): pl.pallas_call(head_kernel, name='head', out_shape=[jax.ShapeDtypeStruct(...  214 us
    pallas_call x1, Pallas kernels, finish(): pl.pallas_call(finish_kernel, name='finish', out_shape=[jax.ShapeDtypeStr...  57.9 us
    pallas_call x1, Pallas kernels, start(): pl.pallas_call(start_kernel, name='start', out_shape=[shape((NDEV, TOK),...  41.7 us
    unnamed x14, local copies, waits for them, and re-layouts  6.64 us

profile of v2, /device:TPU:0, one launch (start us, length us, event | category | flops | bytes accessed | tf_op | source)
XLA Modules:
  0.0 327.5 jit_solution(16235167187413230641)
XLA Ops:
  0.7 0.7 pad_add_fusion
  1.4 0.6 broadcast_in_dim.61.meta
  2.0 41.7 %start.1 = (s32[16,1024]{1,0:T(8,128)S(1)}, s32[8,1,1024]{2,1,0:T(1,128)}, f32[8,1,1024]{2,1,0:T(1,128)}, s32[1,1024]{1,0:T(1,128)}, bf16[1024,256]{1,0:T(8,128)...) custom-call(s32[3,1,1024]{2,1,0:T(1,128)} %broadcast_in_dim.61.meta,, ...), custom_call_target="tpu_custom_call" | custom-call | tf_op jit(solution)/shard_map/start/pallas_call | solution.py:266
  43.7 1.5 convert_reduce_fusion.1
  45.2 0.7 convert_element_type.35.where
  45.9 0.1 add_select_fusion.4
  45.9 0.4 convert_reduce_fusion
  46.3 0.6 reduce_max.9
  47.6 0.2 conditional.2
  47.8 213.9 %head.1 = (f32[256,1024]{1,0:T(8,128)}, f32[3584,256]{1,0:T(8,128)}, f32[1,128]{1,0:T(1,128)}) custom-call(bf16[1024,256]{1,0:T(8,128)(2,1)} %get-tuple-element.194.hn, bf16[3584,256]{1,0:T(8,128)(2,1)} %e_own.1, s32[8,1,1024]{2,1,0:T(1,128)} %get-tuple-element.195.lab, f32[8,1,1024]{2,1,0:T(1,128)} %get-tuple-element.196.coef), custom_call_target="tpu_custom_call" | custom-call | tf_op jit(solution)/shard_map/head/pallas_call | solution.py:760
  261.7 0.0 copy-start.6
  261.7 57.9 %finish.1 = (f32[3584,256]{1,0:T(8,128)}, f32[16,1536]{1,0:T(8,128)}, f32[16,1536]{1,0:T(8,128)}, f32[96,256]{1,0:T(8,128)}, f32[1,128]{1,0:T(1,128)}, /*index=5*/f32[1024,256]{1,0:T(8,128)}) custom-call(s32[1,1024]{1,0:T(1,128)} %get-tuple-element.186.pos, f32[256,1024]{1,0:T(8,128)} %get-tuple-element.197.dhn, bf16[1024,256]{1,0:T(8,128)(2,1)} %get-tuple-element.198.x, ...), custom_call_target="tpu_custom_call" | custom-call | tf_op jit(solution)/shard_map/finish/pallas_call | solution.py:541
  319.7 0.0 copy-done.6
  319.7 0.0 copy-start.9
  319.7 0.5 copy-done.9
  320.3 0.0 copy-start.5
  320.3 0.0 copy-start.4
  320.3 0.0 copy-start.3
  320.3 4.2 %copy.42 = f32[3584,256]{1,0:T(8,128)} copy(f32[3584,256]{1,0:T(8,128)} %get-tuple-element.437) | data formatting | bytes 7340032
  324.5 0.0 copy-done.5
  324.5 0.6 copy.43
  325.1 0.0 copy-done.4
  325.1 0.6 copy.44
  325.8 0.6 copy.45
  (5 shorter events, 0.0 us)
Async XLA Ops:
  261.7 58.0 %copy-start.6 = (s32[1024]{0:T(1024)S(1)}, s32[1024]{0:T(1024)}, u32[]{:S(2)}) copy-start(s32[1024]{0:T(1024)} %param.17) | copy-start | bytes 12292
  319.7 0.6 copy-start.9
  320.3 4.2 %copy-start.5 = (f32[16,1536]{1,0:T(8,128)S(1)}, f32[16,1536]{1,0:T(8,128)}, u32[]{:S(2)}) copy-start(f32[16,1536]{1,0:T(8,128)} %get-tuple-element.433) | copy-start | bytes 294916
  320.3 4.8 %copy-start.4 = (f32[16,1536]{1,0:T(8,128)S(1)}, f32[16,1536]{1,0:T(8,128)}, u32[]{:S(2)}) copy-start(f32[16,1536]{1,0:T(8,128)} %get-tuple-element.434) | copy-start | bytes 294916
  320.3 5.5 %copy-start.3 = (f32[96,256]{1,0:T(8,128)S(1)}, f32[96,256]{1,0:T(8,128)}, u32[]{:S(2)}) copy-start(f32[96,256]{1,0:T(8,128)} %get-tuple-element.435) | copy-start | bytes 294916

commit v3 on v2

--- a/solution.py
+++ b/solution.py
@@ -158,7 +158,7 @@
         upper[128 * r : 128 * r + 128, :] = jnp.where(rows < cols, 1.0, 0.0).astype(BF16)
 
 
-def start_kernel(meta, gate, up, down, table, gain_mlp, gain_head, ids_o, lab_o, coef_o, pos_o, x_o, local, h_o, hn_o, gate_o, up_o, down_o,
+def start_kernel(meta, gate, up, down, table, gain_mlp, gain_head, ids_o, lab_o, coef_o, pos_o, full_o, x_o, local, h_o, hn_o, gate_o, up_o, down_o,
                  meta_all, key, lid, upper, send, recv, total, ms, mr, ws, wr, fs, fr, ss, rs):
     me, chip, core, partner = whereabouts()
     barrier_greet(me)
@@ -229,6 +229,12 @@
     for j in range(NCHIP):
         lab_o[j] = meta_all[2 * j + core, 1] - chip * V_CHIP
         coef_o[j] = meta_all[2 * j + core, 2].astype(F32) / n_all
+
+    full = jnp.zeros((NDEV, 1), F32)
+    for d in range(NDEV):
+        far = ids_o[...] - d * ROWS
+        full = jnp.maximum(full, jnp.sum(jnp.where((far >= 0) & (far < ROWS), 1.0, 0.0), axis=1, keepdims=True))
+    full_o[...] = jnp.broadcast_to(jnp.max(full, axis=0, keepdims=True), full_o.shape).astype(jnp.int32)
 
     first = lax.broadcasted_iota(jnp.int32, (NDEV, TOK), 0) * ROWS
     mine = meta[0]
@@ -267,13 +273,13 @@
         start_kernel,
         name="start",
         out_shape=[
-            shape((NDEV, TOK), jnp.int32), shape((NCHIP, 1, TOK), jnp.int32), shape((NCHIP, 1, TOK), F32), shape((1, TOK), jnp.int32),
+            shape((NDEV, TOK), jnp.int32), shape((NCHIP, 1, TOK), jnp.int32), shape((NCHIP, 1, TOK), F32), shape((1, TOK), jnp.int32), shape((1, 128), jnp.int32),
             shape((TOK, DIM), BF16), shape((NDEV, CAP, 1), F32),
         ]
         + [shape((TOK, DIM), BF16)] * 2
         + [shape((NDEV,) + a.shape, a.dtype) for a in (gate, up, down)],
         in_specs=[VMEM_SPEC] * 7,
-        out_specs=[VMEM_SPEC] * 11,
+        out_specs=[VMEM_SPEC] * 12,
         scratch_shapes=[
             vm((NDEV, 3, 1, TOK), jnp.int32), vm((NDEV, TOK), jnp.int32), vm((NDEV, TOK), jnp.int32), vm((TOK, TOK), BF16),
             vm((NDEV, CAP, DIM), BF16), vm((NDEV, CAP, DIM), BF16), vm((TOK, DIM), F32),
@@ -551,8 +557,8 @@
     )(pos, dhn, x, h, gate, up, down, gain_mlp, gain_head, where, base, loss)
 
 
-def head_kernel(hn, e_own, lab, coef, dhn_o, de_o, loss_o, hn_all, e_full, e_t, d_e, dhn_buf, dhn_recv, stat, stat_recv, lse_own, lse_all, la, lb, da, db,
-                hs, hr, es, er, sts, str_, lss, lsr, ds_, dr, xs, xr):
+def head_kernel(hn, e_own, lab, coef, dhn_o, de_o, loss_o, hn_all, e_full, e_t, d_e, dhn_buf, dhn_recv, stat, stat_all, lse_all, la, lb, da, db,
+                hs, hr, es, er, sts, str_, ds_, dr, xs, xr):
     me, chip, core, partner = whereabouts()
     bar = pltpu.get_barrier_semaphore()
     pl.semaphore_signal(bar, inc=1, device_id=(partner,), device_id_type=MESH)
@@ -603,6 +609,9 @@
             sums[r % 4] = e if sums[r % 4] is None else sums[r % 4] + e
         return top, (sums[0] + sums[1]) + (sums[2] + sums[3])
 
+    def stat_copy(mask, b, slot):
+        return pltpu.make_async_remote_copy(stat.at[b], stat_all.at[slot, b], sts.at[mask, b], str_.at[slot, b], **same_core(flip(chip, mask)))
+
     def keep(g, m, s):
         _, b, n0, t = where_is(g, False)
 
@@ -612,9 +621,10 @@
             tot = jnp.sum(s * jnp.exp2(m - top), axis=0, keepdims=True)
             stat[b, :, pl.ds(n0, NT)] = top + jnp.log(tot) * LOG2E
 
-        @pl.when((lax.rem(g + 1, PER_BLOCK) == 0) & (g >= PER_BLOCK))
+        @pl.when(lax.rem(g + 1, PER_BLOCK) == 0)
         def _():
-            pltpu.make_async_remote_copy(stat.at[b], stat_recv.at[chip], sts.at[b], str_.at[chip], **same_core(b)).start()
+            for mask in MASKS:
+                stat_copy(mask, b, chip).start()
 
     def pass1(i, carry):
         m, s, top_a = carry
@@ -640,7 +650,7 @@
 
     scope = jax.named_scope("stats")
     scope.__enter__()
-    stat_recv[chip] = stat[chip]
+    stat_all[chip] = stat[...]
 
     def clear_de(i, carry):
         d_e[pl.ds(pl.multiple_of(i * COLS, COLS), COLS), :] = jnp.zeros((COLS, DIM), F32)
@@ -652,24 +662,17 @@
         return carry
 
     lax.fori_loop(0, NCHIP, clear_dhn, 0)
-    for mask in MASKS:
-        there = flip(chip, mask)
-        pltpu.make_async_remote_copy(stat.at[there], stat_recv.at[there], sts.at[there], str_.at[there], **same_core(there)).wait_recv()
-    stats = stat_recv[...]
-    top = jnp.max(stats, axis=0)
-    lse_own[...] = top + jnp.log(jnp.sum(jnp.exp2(stats - top[None]), axis=0)) * LOG2E
-
-    def lse_copy(there, slot):
-        return pltpu.make_async_remote_copy(lse_own, lse_all.at[slot], lss.at[there], lsr.at[slot], **same_core(there))
-
-    for mask in MASKS:
-        lse_copy(flip(chip, mask), chip).start()
-    lse_all[chip] = lse_own[...]
     lax.fori_loop(0, V_CHIP // COLS, clear_de, 0)
-    for mask in MASKS:
-        there = flip(chip, mask)
-        lse_copy(there, there).wait_recv()
-
+
+    def stat_wait(n, carry):
+        mask = lax.div(n, NCHIP)
+        stat_copy(mask, lax.rem(n, NCHIP), flip(chip, mask)).wait_recv()
+        return carry
+
+    lax.fori_loop(NCHIP, NCHIP * NCHIP, stat_wait, 0)
+    stats = [stat_all[j] for j in range(NCHIP)]
+    top = functools.reduce(jnp.maximum, stats)
+    lse_all[...] = top + jnp.log(sum(jnp.exp2(one - top) for one in stats)) * LOG2E
     scope.__exit__(None, None, None)
 
     iota = lax.broadcasted_iota(jnp.int32, (16, NT), 0)
@@ -693,8 +696,8 @@
     def products(g, d):
         k, b, n0, t = where_is(g, True)
         rows = pl.ds(pl.multiple_of(t * TV, TV), TV)
+        dhn_buf[k, :, pl.ds(n0, NT)] += jnp.dot(e_t[:, rows], d[...], preferred_element_type=F32)
         d_e[rows, :] += jnp.dot(d[...], hn_all[b, pl.ds(n0, NT), :], preferred_element_type=F32)
-        dhn_buf[k, :, pl.ds(n0, NT)] += jnp.dot(e_t[:, rows], d[...], preferred_element_type=F32)
 
     def dhn_copy(k, there, slot):
         return pltpu.make_async_remote_copy(dhn_buf.at[k], dhn_recv.at[slot], ds_.at[k], dr.at[slot], **same_core(there))
@@ -729,7 +732,7 @@
         return pltpu.make_async_remote_copy(d_e.at[rows], de_o, xs, xr, device_id=(partner,), device_id_type=MESH)
 
     de_copy(theirs).start()
-    own = jnp.sum(coef[chip] * lse_own[...] * LN2, axis=1, keepdims=True)
+    own = jnp.sum(coef[chip] * lse_all[chip] * LN2, axis=1, keepdims=True)
     picked = jnp.sum(jnp.sum(picked, axis=0, keepdims=True), axis=1, keepdims=True)
     loss_o[...] = jnp.broadcast_to(own - picked, loss_o.shape)
     with jax.named_scope("dhn_wait"):
@@ -747,8 +750,8 @@
     for mask in MASKS:
         there = flip(chip, mask)
         hn_copy(there, chip).wait_send()
-        pltpu.make_async_remote_copy(stat.at[there], stat_recv.at[chip], sts.at[there], str_.at[chip], **same_core(there)).wait_send()
-        lse_copy(there, chip).wait_send()
+        for b in range(NCHIP):
+            stat_copy(mask, b, chip).wait_send()
         dhn_copy(7 - mask, there, chip).wait_send()
 
 
@@ -766,10 +769,10 @@
         scratch_shapes=[
             vm((NCHIP, TOK, DIM), BF16), vm((V_CHIP, DIM), BF16), vm((DIM, V_CHIP), BF16), vm((V_CHIP, DIM), F32),
             vm((NCHIP, DIM, TOK), F32), vm((NCHIP, DIM, TOK), F32),
-            vm((NCHIP, 1, TOK), F32), vm((NCHIP, 1, TOK), F32), vm((1, TOK), F32), vm((NCHIP, 1, TOK), F32),
+            vm((NCHIP, 1, TOK), F32), vm((NCHIP, NCHIP, 1, TOK), F32), vm((NCHIP, 1, TOK), F32),
             vm((TV, NT), F32), vm((TV, NT), F32), vm((TV, NT), BF16), vm((TV, NT), BF16),
         ]
-        + eight + one + eight + eight + eight + one,
+        + eight + one + [dma((NCHIP, NCHIP))] * 2 + eight + one,
         compiler_params=params(4, 63),
     )(hn, table, lab, coef)
 
@@ -788,11 +791,10 @@
     def device_step(tok_ids, tok_labels, loss_mask, table, gain_mlp, gain_head, gate_shard, up_shard, down_shard):
         meta = jnp.stack([tok_ids, tok_labels, loss_mask])[:, None, :]
         gains = (gain_mlp[None], gain_head[None])
-        ids_all, lab_rel, coef, pos, emb_rows, local, *acts, gate_full, up_full, down_full = start(meta, gate_shard, up_shard, down_shard, table, *gains)
+        ids_all, lab_rel, coef, pos, full, emb_rows, local, *acts, gate_full, up_full, down_full = start(meta, gate_shard, up_shard, down_shard, table, *gains)
 
         devices = jnp.arange(NDEV, dtype=jnp.int32)
-        counts = jnp.sum(((ids_all // ROWS)[:, None, :] == devices[None, :, None]).astype(jnp.int32), axis=2)
-        rounds = (jnp.max(counts) + CAP - 1) // CAP
+        rounds = (full[0, 0] + CAP - 1) // CAP
         slots = jnp.arange(NDEV * CAP, dtype=jnp.int32)
 
         def places(ids_all, tok_ids):

time: 328 us -> 324 us (0.988)
  no operation moved by 1% of the time
where the time goes in v3:
time: 324 us
  Pallas kernels  311 us (96%)
  local copies, waits for them, and re-layouts  8.03 us (2%)
    pallas_call x1, Pallas kernels, head(): pl.pallas_call(head_kernel, name='head', out_shape=[jax.ShapeDtypeStruct(...  211 us
    pallas_call x1, Pallas kernels, finish(): pl.pallas_call(finish_kernel, name='finish', out_shape=[jax.ShapeDtypeStr...  58 us
    pallas_call x1, Pallas kernels, start(): pl.pallas_call(start_kernel, name='start', out_shape=[shape((NDEV, TOK),...  41.7 us
    unnamed x14, local copies, waits for them, and re-layouts  6.74 us

profile of v3, /device:TPU:0, one launch (start us, length us, event | category | flops | bytes accessed | tf_op | source)
XLA Modules:
  0.0 324.2 jit_solution(17671008726495693156)
XLA Ops:
  0.7 0.7 pad_add_fusion
  1.4 0.6 broadcast_in_dim.59.meta
  2.0 41.7 %start.1 = (s32[16,1024]{1,0:T(8,128)S(1)}, s32[8,1,1024]{2,1,0:T(1,128)}, f32[8,1,1024]{2,1,0:T(1,128)}, s32[1,1024]{1,0:T(1,128)}, s32[1,128]{1,0:T(1,128)}, /...) custom-call(s32[3,1,1024]{2,1,0:T(1,128)} %broadcast_in_dim.59.meta,, ...), custom_call_target="tpu_custom_call" | custom-call | tf_op jit(solution)/shard_map/start/pallas_call | solution.py:272
  44.4 0.2 conditional.2
  44.6 1.5 convert_reduce_fusion
  46.1 0.7 convert_element_type.31.where
  46.8 211.5 %head.1 = (f32[256,1024]{1,0:T(8,128)}, f32[3584,256]{1,0:T(8,128)}, f32[1,128]{1,0:T(1,128)}) custom-call(bf16[1024,256]{1,0:T(8,128)(2,1)} %get-tuple-element.196.hn, bf16[3584,256]{1,0:T(8,128)(2,1)} %e_own.1, s32[8,1,1024]{2,1,0:T(1,128)} %get-tuple-element.197.lab, f32[8,1,1024]{2,1,0:T(1,128)} %get-tuple-element.198.coef), custom_call_target="tpu_custom_call" | custom-call | tf_op jit(solution)/shard_map/head/pallas_call | solution.py:763
  258.2 0.0 copy-start.6
  258.2 58.0 %finish.1 = (f32[3584,256]{1,0:T(8,128)}, f32[16,1536]{1,0:T(8,128)}, f32[16,1536]{1,0:T(8,128)}, f32[96,256]{1,0:T(8,128)}, f32[1,128]{1,0:T(1,128)}, /*index=5*/f32[1024,256]{1,0:T(8,128)}) custom-call(s32[1,1024]{1,0:T(1,128)} %get-tuple-element.187.pos, f32[256,1024]{1,0:T(8,128)} %get-tuple-element.199.dhn, bf16[1024,256]{1,0:T(8,128)(2,1)} %get-tuple-element.200.x, ...), custom_call_target="tpu_custom_call" | custom-call | tf_op jit(solution)/shard_map/finish/pallas_call | solution.py:547
  316.2 0.0 copy-done.6
  316.2 0.0 copy-start.9
  316.3 0.6 copy-done.9
  316.9 0.0 copy-start.5
  316.9 0.0 copy-start.4
  317.0 0.0 copy-start.3
  317.0 4.2 %copy.42 = f32[3584,256]{1,0:T(8,128)} copy(f32[3584,256]{1,0:T(8,128)} %get-tuple-element.439) | data formatting | bytes 7340032
  321.1 0.0 copy-done.5
  321.1 0.6 copy.43
  321.8 0.0 copy-done.4
  321.8 0.6 copy.44
  322.4 0.0 copy-done.3
  322.4 0.6 copy.45
  (4 shorter events, 0.0 us)
Async XLA Ops:
  258.2 58.0 %copy-start.6 = (s32[1024]{0:T(1024)S(1)}, s32[1024]{0:T(1024)}, u32[]{:S(2)}) copy-start(s32[1024]{0:T(1024)} %param.17) | copy-start | bytes 12292
  316.2 0.7 copy-start.9
  316.9 4.2 %copy-start.5 = (f32[16,1536]{1,0:T(8,128)S(1)}, f32[16,1536]{1,0:T(8,128)}, u32[]{:S(2)}) copy-start(f32[16,1536]{1,0:T(8,128)} %get-tuple-element.435) | copy-start | bytes 294916
  316.9 4.8 %copy-start.4 = (f32[16,1536]{1,0:T(8,128)S(1)}, f32[16,1536]{1,0:T(8,128)}, u32[]{:S(2)}) copy-start(f32[16,1536]{1,0:T(8,128)} %get-tuple-element.436) | copy-start | bytes 294916
  317.0 5.5 %copy-start.3 = (f32[96,256]{1,0:T(8,128)S(1)}, f32[96,256]{1,0:T(8,128)}, u32[]{:S(2)}) copy-start(f32[96,256]{1,0:T(8,128)} %get-tuple-element.437) | copy-start | bytes 294916
